TPU v7x, 128 devices: a whole 4x4x4 slice. The times are simulated.
128 devices in a mesh: gx: 8 (over z, core), gy: 16 (over x, y).
Axes of the slice: x: 4, y: 4, z: 4, core: 2. Of those that a mesh axis runs over, the one named last changes fastest.
Arguments:
- prolong: bfloat16 [8192, 24, 128], P(('gx', 'gy')), may hold values from -0.5 to 0.5
- stiffness: bfloat16 [16384, 4, 128, 128], P(('gx', 'gy')), may hold values from -6 to 6
- request: int32 [16384], P(('gx', 'gy')), may hold values from 0 to 63, as said below
- col_slot: int32 [16384, 4], P(('gx', 'gy')), may hold values from 0 to 127
- col_pos: int32 [16384, 4], P(('gx', 'gy')), may hold values from 0 to 15, as said below
- coarse_owner: int32 [8192, 1], P(('gx', 'gy')), may hold values from 0 to 127; in each aligned block of 64 rows (0 to 63, 64 to 127, ...) no two rows name the same one
Outputs:
- coarse: float32 [16384, 24, 384], P(('gx', 'gy'))
Inputs may be any that keep to these rules, and one draw needn't show every extreme that they name: `request`: on each device, entries k * 1 to (k + 1) * 1 - 1 name distinct aggregates of device k, as local indices there. `col_pos`: the 4 entries of one block row are distinct. `coarse_owner`: among one device's 64 aggregates at most 1 share a coarse owner, and on some devices 1 do.
All inputs are finite; a program needn't handle non-finite values.
Results may differ from a plain program's by a relative error of at most 0.0003.
Values may be sent and summed in bfloat16 or wider, within the bound.
A program may use at most 128 MiB of HBM per device.

v0:
```python
import functools

import jax
import jax.numpy as jnp
from jax import lax
from jax.experimental import pallas as pl
from jax.experimental.pallas import tpu as pltpu
from jax.sharding import PartitionSpec as P

MAXNB = 16
AXES = ("gx", "gy")
LANES = 128
TOP = 32767.0
MESH = pl.DeviceIdType.MESH
HBM = pl.BlockSpec(memory_space=pl.ANY)
VMEM = pl.BlockSpec(memory_space=pltpu.VMEM)
SMEM = pl.BlockSpec(memory_space=pltpu.SMEM)
NT = (((1,), (1,)), ((), ()))


def peer_at(k, gx, gy, mixed):
    n = gx * gy
    x, y = lax.axis_index("gx"), lax.axis_index("gy")
    if gx % 2:
        return lax.rem(x * gy + y + 1 + k, n)
    half = gx // 2
    count = half * gy
    if mixed:
        near, i = lax.rem(k, 2), k // 2
    else:
        near, i = k // count, lax.rem(k, count)
    i = lax.rem(i + near, count)
    side = lax.rem(x // half + 1 + near, 2)
    row = side * half + lax.rem(x + i // gy, half)
    return row * gy + lax.rem(y + i, gy)


def deliver_kernel(dims, code_ref, scale_ref, out_ref, land_ref, land_scale, wide_ref, *sems):
    gx, gy, cv = dims
    code_send, code_recv, scale_send, scale_recv, out_sem = sems
    n, rows, width = code_ref.shape
    take = rows // cv
    me = lax.axis_index("gx") * gy + lax.axis_index("gy")
    barrier = pltpu.get_barrier_semaphore()

    def where(peer):
        return (peer // gy, lax.rem(peer, gy))

    def greet(k, c):
        peer = peer_at(k, gx, gy, True)
        pl.semaphore_signal(barrier, inc=1, device_id=where(peer), device_id_type=MESH)
        return c

    lax.fori_loop(0, n - 1, greet, 0)

    def copies(peer, source):
        return [
            pltpu.make_async_remote_copy(
                src_ref=src.at[peer], dst_ref=dst.at[source],
                send_sem=send.at[peer], recv_sem=recv.at[source],
                device_id=where(peer), device_id_type=MESH,
            )
            for src, dst, send, recv in (
                (scale_ref, land_scale, scale_send, scale_recv),
                (code_ref, land_ref, code_send, code_recv),
            )
        ]

    def out_copy(p):
        at = pl.ds(p * take, take)
        return pltpu.make_async_copy(wide_ref.at[at], out_ref.at[at], out_sem.at[p])

    pl.semaphore_wait(barrier, n - 1)

    def send(k, c):
        for copy in copies(peer_at(k, gx, gy, True), me):
            copy.start()
        return c

    lax.fori_loop(0, n - 1, send, 0)

    def decode(code, scale, p):
        values = code.astype(jnp.int32).astype(jnp.float32) * as_column(scale, rows)
        wide_ref[pl.ds(p * take, take)] = values.reshape(take, cv, width)
        out_copy(p).start()

    decode(code_ref[me], scale_ref[me], me)

    def drain(k, c):
        source = peer_at(k, gx, gy, True)
        for copy in copies(source, source):
            copy.wait()
        decode(land_ref[source], land_scale[source], source)
        return c

    lax.fori_loop(0, n - 1, drain, 0)

    def finish(p, c):
        out_copy(p).wait()
        return c

    lax.fori_loop(0, n, finish, 0)


def delivered(code, scale, cv, gx, gy):
    n, rows, width = code.shape
    sem = pltpu.SemaphoreType.DMA
    out = (n * rows // cv, cv, width)
    return pl.pallas_call(
        functools.partial(deliver_kernel, (gx, gy, cv)),
        out_shape=jax.ShapeDtypeStruct(out, jnp.float32),
        in_specs=[VMEM, VMEM],
        out_specs=HBM,
        scratch_shapes=[
            pltpu.VMEM(code.shape, jnp.int16),
            pltpu.VMEM(scale.shape, jnp.float32),
            pltpu.VMEM(out, jnp.float32),
        ]
        + [sem((n,))] * 5,
        compiler_params=pltpu.CompilerParams(
            collective_id=4, has_side_effects=True, vmem_limit_bytes=40 << 20
        ),
        name="delivered",
    )(code, scale)


def exchange_kernel(gx, gy, count, *refs):
    ins, outs = refs[:count], refs[count : 2 * count]
    send_sem, recv_sem, local_sem = refs[2 * count :]
    n = gx * gy
    me = lax.axis_index("gx") * gy + lax.axis_index("gy")
    barrier = pltpu.get_barrier_semaphore()

    def greet(k, c):
        peer = lax.rem(me + k, n)
        pl.semaphore_signal(barrier, inc=1, device_id=(peer // gy, lax.rem(peer, gy)), device_id_type=MESH)
        return c

    lax.fori_loop(1, n, greet, 0)
    own = [pltpu.make_async_copy(ins[i].at[me], outs[i].at[me], local_sem.at[i]) for i in range(count)]
    for copy in own:
        copy.start()
    pl.semaphore_wait(barrier, n - 1)

    def copies(k, source):
        peer = lax.rem(me + k, n)
        return [
            pltpu.make_async_remote_copy(
                src_ref=ins[i].at[peer],
                dst_ref=outs[i].at[source],
                send_sem=send_sem.at[i, k],
                recv_sem=recv_sem.at[i, k],
                device_id=(peer // gy, lax.rem(peer, gy)),
                device_id_type=MESH,
            )
            for i in range(count)
        ]

    def send(k, c):
        for copy in copies(k, me):
            copy.start()
        return c

    lax.fori_loop(1, n, send, 0)

    def drain(k, c):
        for copy in copies(k, lax.rem(me + n - k, n)):
            copy.wait()
        return c

    lax.fori_loop(1, n, drain, 0)
    for copy in own:
        copy.wait()


def exchange(arrays, gx, gy, number):
    count = len(arrays)
    n = gx * gy
    return pl.pallas_call(
        functools.partial(exchange_kernel, gx, gy, count),
        out_shape=[jax.ShapeDtypeStruct(a.shape, a.dtype) for a in arrays],
        in_specs=[HBM] * count,
        out_specs=[HBM] * count,
        scratch_shapes=[
            pltpu.SemaphoreType.DMA((count, n)),
            pltpu.SemaphoreType.DMA((count, n)),
            pltpu.SemaphoreType.DMA((count,)),
        ],
        compiler_params=pltpu.CompilerParams(collective_id=number, has_side_effects=True),
        name=f"exchange{number}",
    )(*arrays)


def as_row(column):
    rows = column.shape[0]
    shape = (rows, LANES)
    eye = lax.broadcasted_iota(jnp.int32, shape, 0) == lax.broadcasted_iota(jnp.int32, shape, 1)
    return jnp.sum(jnp.where(eye, column, 0.0), axis=0, keepdims=True)


def as_column(row, rows):
    shape = (rows, LANES)
    eye = lax.broadcasted_iota(jnp.int32, shape, 0) == lax.broadcasted_iota(jnp.int32, shape, 1)
    return jnp.sum(jnp.where(eye, row, 0.0), axis=1, keepdims=True)


def coded(values):
    top = jnp.maximum(jnp.max(jnp.abs(values), axis=1, keepdims=True), 1e-30)
    code = jnp.round(values * (TOP / top)).astype(jnp.int32).astype(jnp.int16)
    return code, as_row(top * (1.0 / TOP))


def group_product(dims, grp, slot_ref, wide_ref, cols_ref, mats_of):
    cv, bps, group = dims
    dof = wide_ref.shape[-1]
    span = bps * cv
    lane = lax.broadcasted_iota(jnp.int32, (dof, LANES), 1)
    applied = []
    for tl in range(group):
        for q in range(bps):
            block = wide_ref[slot_ref[grp * group + tl, q]]
            at = (span * tl + cv * q) % LANES
            first = min(cv, LANES - at)
            cols_ref[tl, at : at + first, :] = block[:first]
            if first < cv:
                cols_ref[tl, 0 : cv - first, :] = block[first:]
    for tl in range(group):
        cols = cols_ref[tl].astype(jnp.bfloat16)
        mats = mats_of(tl).reshape(bps * dof, dof)
        prod = lax.dot_general(mats, cols, NT, preferred_element_type=jnp.float32)
        rel = (lane + (LANES * tl - span * tl) % LANES) % LANES
        one = prod[(bps - 1) * dof :]
        for q in range(bps - 2, -1, -1):
            one = jnp.where(rel < cv * (q + 1), prod[q * dof : (q + 1) * dof], one)
        applied.append(one)
    tiles = []
    for j in range(span * group // LANES):
        low, high = LANES * j // span, (LANES * (j + 1) - 1) // span
        tile = applied[high]
        for tl in range(high - 1, low - 1, -1):
            tile = jnp.where(lane < span * (tl + 1) - LANES * j, applied[tl], tile)
        tiles.append(tile)
    whole = jnp.concatenate(tiles, axis=1)
    hi = whole.astype(jnp.bfloat16)
    lo = (whole - hi.astype(jnp.float32)).astype(jnp.bfloat16)
    rows = wide_ref[pl.ds(grp * group, group)].reshape(group * cv, dof).astype(jnp.bfloat16)
    both = jnp.dot(rows, hi, preferred_element_type=jnp.float32) + jnp.dot(
        rows, lo, preferred_element_type=jnp.float32
    )
    wide_lane = lax.broadcasted_iota(jnp.int32, (cv, span * group), 1)
    out = both[(group - 1) * cv :]
    for tl in range(group - 2, -1, -1):
        out = jnp.where(wide_lane < span * (tl + 1), both[tl * cv : (tl + 1) * cv], out)
    return out


def product_kernel(dims, slot_ref, fetched_ref, stiff_ref, out_ref, wide_ref, cols_ref):
    cv, bps, group, per_step = dims
    step = pl.program_id(0)

    @pl.when(step == 0)
    def _():
        wide_ref[...] = fetched_ref[...].astype(jnp.float32)

    def body(k, c):
        out_ref[k] = group_product(
            (cv, bps, group), step * per_step + k, slot_ref, wide_ref, cols_ref,
            lambda tl: stiff_ref[k * group + tl],
        )
        return c

    lax.fori_loop(0, per_step, body, 0)


def products(fetched, stiffness, col_slot, group):
    slots, cv, dof = fetched.shape
    bps = stiffness.shape[1]
    groups = slots // group
    per_step = 4 if groups % 4 == 0 else 1
    width = group * bps * cv
    return pl.pallas_call(
        functools.partial(product_kernel, (cv, bps, group, per_step)),
        grid=(groups // per_step,),
        out_shape=jax.ShapeDtypeStruct((groups, cv, width), jnp.float32),
        in_specs=[
            SMEM,
            pl.BlockSpec((slots, cv, dof), lambda i: (0, 0, 0)),
            pl.BlockSpec((per_step * group, bps, dof, dof), lambda i: (i, 0, 0, 0)),
        ],
        out_specs=pl.BlockSpec((per_step, cv, width), lambda i: (i, 0, 0)),
        scratch_shapes=[
            pltpu.VMEM((slots, cv, dof), jnp.float32),
            pltpu.VMEM((group, LANES, dof), jnp.float32),
        ],
        compiler_params=pltpu.CompilerParams(vmem_limit_bytes=48 << 20),
        name="products",
    )(col_slot, fetched, stiffness)


def fused_kernel(
    dims,
    slot_ref, meta_ref, prolong_ref, stiff_ref,
    meta_out, part_out, scale_out,
    req_ref, stage_ref, fetched_ref, wide_ref, cols_ref, mats_ref, code_ref, factor_ref,
    meta_send, meta_recv, fetch_send, fetch_recv, part_send, part_recv, scale_send, scale_recv,
    mats_sem, own_sem,
):
    gx, gy, cv, bps, group = dims
    n = gx * gy
    me = lax.axis_index("gx") * gy + lax.axis_index("gy")
    barrier = pltpu.get_barrier_semaphore()

    def where(peer):
        return (peer // gy, lax.rem(peer, gy))

    def remote(src, dst, send_sem, recv_sem, peer):
        return pltpu.make_async_remote_copy(
            src_ref=src, dst_ref=dst, send_sem=send_sem, recv_sem=recv_sem,
            device_id=where(peer), device_id_type=MESH,
        )

    def meta_copy(peer, source):
        return remote(
            meta_ref.at[peer], meta_out.at[source], meta_send.at[peer], meta_recv.at[source], peer
        )

    def fetch_copy(peer, source):
        return remote(
            stage_ref.at[pl.ds(peer * group, group)],
            fetched_ref.at[pl.ds(source * group, group)],
            fetch_send.at[peer], fetch_recv.at[source], peer,
        )

    def part_copies(peer, source):
        return (
            remote(code_ref.at[peer], part_out.at[source], part_send.at[peer], part_recv.at[source], peer),
            remote(
                factor_ref.at[peer], scale_out.at[source], scale_send.at[peer], scale_recv.at[source], peer
            ),
        )

    def mats_copy(peer):
        return pltpu.make_async_copy(
            stiff_ref.at[pl.ds(peer * group, group)],
            mats_ref.at[pl.ds(peer * group, group)],
            mats_sem.at[peer],
        )

    def greet(k, c):
        pl.semaphore_signal(barrier, inc=1, device_id=where(lax.rem(me + k, n)), device_id_type=MESH)
        return c

    lax.fori_loop(1, n, greet, 0)
    own_meta = pltpu.make_async_copy(meta_ref.at[me], meta_out.at[me], own_sem.at[0])
    own_meta.start()

    def load(k, c):
        mats_copy(peer_at(k, gx, gy, False)).start()
        return c

    lax.fori_loop(0, n, load, 0)
    pl.semaphore_wait(barrier, n - 1)

    def ask(k, c):
        meta_copy(peer_at(k, gx, gy, True), me).start()
        return c

    lax.fori_loop(0, n - 1, ask, 0)
    own_meta.wait()

    def asked(k, c):
        source = peer_at(k, gx, gy, True)
        meta_copy(source, source).wait()
        return c

    lax.fori_loop(0, n - 1, asked, 0)
    to_scalars = pltpu.make_async_copy(meta_out, req_ref, own_sem.at[1])
    to_scalars.start()
    to_scalars.wait()

    def fill(k, c):
        peer = peer_at(k, gx, gy, True)
        for j in range(group):
            stage_ref[peer * group + j] = prolong_ref[req_ref[peer, 0, j]]
        return c

    lax.fori_loop(0, n, fill, 0)

    def answer(k, c):
        fetch_copy(peer_at(k, gx, gy, True), me).start()
        return c

    lax.fori_loop(0, n - 1, answer, 0)
    for j in range(group):
        wide_ref[me * group + j] = stage_ref[me * group + j].astype(jnp.float32)

    def take(k, c):
        source = peer_at(k, gx, gy, True)
        fetch_copy(source, source).wait()
        for j in range(group):
            wide_ref[source * group + j] = fetched_ref[source * group + j].astype(jnp.float32)
        return c

    lax.fori_loop(0, n - 1, take, 0)
    wide_step = 2 if n % 2 == 0 else 1

    def work(i, c):
        for u in range(wide_step):
            mats_copy(peer_at(i * wide_step + u, gx, gy, False)).wait()
        for u in range(wide_step):
            peer = peer_at(i * wide_step + u, gx, gy, False)
            out = group_product(
                (cv, bps, group), peer, slot_ref, wide_ref, cols_ref.at[u],
                lambda tl: mats_ref[peer * group + tl],
            )
            code_ref[peer], factor_ref[peer] = coded(out)

        @pl.when(i > 0)
        def _():
            for u in range(wide_step):
                for copy in part_copies(peer_at((i - 1) * wide_step + u, gx, gy, False), me):
                    copy.start()

        return c

    lax.fori_loop(0, n // wide_step, work, 0)
    for k in range(n - wide_step, n - 1):
        for copy in part_copies(peer_at(k, gx, gy, False), me):
            copy.start()
    own = (
        pltpu.make_async_copy(code_ref.at[me], part_out.at[me], own_sem.at[2]),
        pltpu.make_async_copy(factor_ref.at[me], scale_out.at[me], own_sem.at[3]),
    )
    for copy in own:
        copy.start()

    def drain(k, c):
        source = peer_at(k, gx, gy, False)
        for copy in part_copies(source, source):
            copy.wait()
        return c

    lax.fori_loop(0, n - 1, drain, 0)
    for copy in own:
        copy.wait()


def fused(meta, prolong, stiffness, col_slot, gx, gy, group):
    slots, bps, dof, _ = stiffness.shape
    cv = prolong.shape[1]
    n = gx * gy
    width = group * bps * cv
    sem = pltpu.SemaphoreType.DMA
    return pl.pallas_call(
        functools.partial(fused_kernel, (gx, gy, cv, bps, group)),
        out_shape=[
            jax.ShapeDtypeStruct(meta.shape, jnp.int32),
            jax.ShapeDtypeStruct((n, cv, width), jnp.int16),
            jax.ShapeDtypeStruct((n, 1, LANES), jnp.float32),
        ],
        in_specs=[SMEM, VMEM, VMEM, HBM],
        out_specs=[VMEM, VMEM, VMEM],
        scratch_shapes=[
            pltpu.SMEM(meta.shape, jnp.int32),
            pltpu.VMEM((slots, cv, dof), jnp.bfloat16),
            pltpu.VMEM((slots, cv, dof), jnp.bfloat16),
            pltpu.VMEM((slots, cv, dof), jnp.float32),
            pltpu.VMEM((2, group, LANES, dof), jnp.float32),
            pltpu.VMEM((slots, bps, dof, dof), jnp.bfloat16),
            pltpu.VMEM((n, cv, width), jnp.int16),
            pltpu.VMEM((n, 1, LANES), jnp.float32),
        ]
        + [sem((n,))] * 9
        + [sem((4,))],
        compiler_params=pltpu.CompilerParams(
            collective_id=1, has_side_effects=True, vmem_limit_bytes=56 << 20
        ),
        name="fused",
    )(col_slot, meta, prolong, stiffness)


def gather_rows_kernel(dims, meta_ref, owner_ref, part_ref, *refs):
    cv, bps, per_peer, group, send_max, quant = dims
    if quant:
        scale_ref, out_ref, out_scale_ref, total_ref, place_ref, seen_ref = refs
    else:
        out_ref, out_scale_ref, total_ref, place_ref, seen_ref = refs
    n = out_ref.shape[0]
    groups, _, width = part_ref.shape
    span = width // group
    total_ref[...] = jnp.zeros_like(total_ref)

    def clear(i, c):
        seen_ref[i] = 0
        return c

    lax.fori_loop(0, n, clear, 0)

    def rank(a, c):
        owner = owner_ref[a]
        before = seen_ref[owner]
        place_ref[a] = owner * send_max + before
        seen_ref[owner] = before + 1
        return c

    lax.fori_loop(0, owner_ref.shape[0], rank, 0)
    lane = lax.broadcasted_iota(jnp.int32, (cv, width), 1)
    column = lax.broadcasted_iota(jnp.int32, (width, width), 0)
    row_lane = lax.broadcasted_iota(jnp.int32, (1, width), 1)

    def body(g, c):
        at = row_lane
        for j in range(group * bps):
            t = g * group + j // bps
            pos = meta_ref[t // per_peer, 0, per_peer + (t % per_peer) * bps + j % bps]
            at = at + jnp.where(row_lane // cv == j, cv * (pos - j), 0)
        hot = jnp.where(column == at, 1.0, 0.0).astype(jnp.bfloat16)
        if quant:
            code = part_ref[g].astype(jnp.int32)
            high = code >> 8
            pieces = [high.astype(jnp.float32), (code - high * 256).astype(jnp.float32)]
            weights = [256.0, 1.0]
        else:
            rest = part_ref[g]
            pieces, weights = [], [1.0, 1.0, 1.0]
            for _ in range(3):
                piece = rest.astype(jnp.bfloat16).astype(jnp.float32)
                pieces.append(piece)
                rest = rest - piece
        placed = 0.0
        for piece, weight in zip(pieces, weights):
            stack = jnp.concatenate(
                [
                    jnp.where((lane >= span * tl) & (lane < span * (tl + 1)), piece, 0.0)
                    for tl in range(group)
                ],
                axis=0,
            ).astype(jnp.bfloat16)
            placed = placed + weight * lax.dot_general(
                stack, hot, NT, preferred_element_type=jnp.float32
            )
        if quant:
            factor = as_column(scale_ref[g], cv)
        for tl in range(group):
            t = g * group + tl
            where = place_ref[meta_ref[t // per_peer, 0, t % per_peer]]
            rows = placed[tl * cv : (tl + 1) * cv]
            if quant:
                rows = rows * factor
            total_ref[where] = total_ref[where] + rows
        return c

    lax.fori_loop(0, groups, body, 0, unroll=4)

    def emit(p, c):
        rows = total_ref[pl.ds(p * send_max, send_max)].reshape(send_max * cv, width)
        out_ref[p], out_scale_ref[p] = coded(rows)
        return c

    lax.fori_loop(0, n, emit, 0, unroll=4)


def gathered_rows(part, scale, meta, owners, n, send_max, group, bps, per_peer):
    groups, cv, width = part.shape
    quant = scale is not None
    args = [meta, owners, part] + ([scale] if quant else [])
    return pl.pallas_call(
        functools.partial(gather_rows_kernel, (cv, bps, per_peer, group, send_max, quant)),
        out_shape=[
            jax.ShapeDtypeStruct((n, send_max * cv, width), jnp.int16),
            jax.ShapeDtypeStruct((n, 1, LANES), jnp.float32),
        ],
        in_specs=[SMEM, SMEM] + [VMEM] * (len(args) - 2),
        out_specs=[VMEM, VMEM],
        scratch_shapes=[
            pltpu.VMEM((n * send_max, cv, width), jnp.float32),
            pltpu.SMEM((owners.shape[0],), jnp.int32),
            pltpu.SMEM((n,), jnp.int32),
        ],
        compiler_params=pltpu.CompilerParams(vmem_limit_bytes=48 << 20),
        name="gathered_rows",
    )(*args)


def per_device(gx, gy, prolong, stiffness, request, col_slot, col_pos, coarse_owner):
    n = gx * gy
    own_aggs, cv, dof = prolong.shape
    slots, bps = col_slot.shape
    per_peer = slots // n
    group = MAXNB // bps
    quant = per_peer == group
    send_max = (2 * own_aggs + n - 1) // n

    meta = jnp.concatenate([request.reshape(n, per_peer), col_pos.reshape(n, per_peer * bps)], axis=1)
    meta = jnp.pad(meta, ((0, 0), (0, LANES - meta.shape[1])))[:, None, :]
    if quant:
        meta_in, part, scale = fused(meta, prolong, stiffness, col_slot, gx, gy, group)
    else:
        (meta_in,) = exchange([meta], gx, gy, 1)
        answer = prolong[meta_in[:, 0, :per_peer].reshape(-1)].reshape(n, per_peer * cv, dof)
        (fetched,) = exchange([answer], gx, gy, 2)
        made = products(fetched.reshape(slots, cv, dof), stiffness, col_slot, group)
        flat = made.reshape(slots // group, cv, group, bps * cv).transpose(0, 2, 1, 3)
        (flat,) = exchange([flat.reshape(n, per_peer * cv, bps * cv)], gx, gy, 3)
        flat = flat.reshape(slots // group, group, cv, bps * cv).transpose(0, 2, 1, 3)
        part, scale = flat.reshape(slots // group, cv, group * bps * cv), None
    code, factor = gathered_rows(
        part, scale, meta_in, coarse_owner[:, 0], n, send_max, group, bps, per_peer
    )
    return delivered(code, factor, cv, gx, gy)


def solution(mesh):
    gx, gy = mesh.shape["gx"], mesh.shape["gy"]
    placed = (
        P(AXES, None, None),
        P(AXES, None, None, None),
        P(AXES),
        P(AXES, None),
        P(AXES, None),
        P(AXES, None),
    )
    return jax.shard_map(
        functools.partial(per_device, gx, gy),
        mesh=mesh,
        in_specs=placed,
        out_specs=P(AXES, None, None),
        check_vma=False,
    )
```

profile of v0, /device:TPU:1, one launch (start us, length us, event | category | flops | bytes accessed | tf_op | source)
XLA Modules:
  0.0 181.9 jit_solution(3182247209262487427)
XLA Ops:
  0.0 0.0 copy-start
  0.0 0.7 pad_add_fusion
  0.7 0.1 copy.15
  0.9 0.6 pad.4
  1.5 20.0 %exchange1.1.meta_ref = s32[128,1,128]{2,1,0:T(1,128)} custom-call(s32[128,1,128]{2,1,0:T(1,128)} %bitcast.16), custom_call_target="tpu_custom_call" | custom-call | tf_op jit(solution)/shard_map/exchange1/pallas_call | solution.py:179
  21.5 3.3 %slice_reduce_fusion = s32[128]{0:T(128)S(1)} fusion(s32[128,1,128]{2,1,0:T(1,128)} %exchange1.1.meta_ref), kind=kLoop, calls=%fused_computation.3 | loop fusion | bytes 1024 | tf_op jit(solution)/shard_map/slice | solution.py:600
  24.8 0.8 copy.16.slot_ref
  25.6 0.0 copy-done
  25.6 1.6 gather_fusion
  27.1 21.4 %exchange2.1.fetched_ref = bf16[128,24,128]{2,1,0:T(8,128)(2,1)} custom-call(bf16[128,24,128]{2,1,0:T(8,128)(2,1)} %gather_fusion), custom_call_target="tpu_custom_call" | custom-call | tf_op jit(solution)/shard_map/exchange2/pallas_call | solution.py:179
  48.5 0.0 copy-start.1
  48.5 1.1 copy-done.1
  49.7 17.7 %products.1 = f32[32,24,384]{2,1,0:T(8,128)S(1)} custom-call(s32[128,4]{1,0:T(8,128)S(1)} %copy.16.slot_ref, bf16[128,24,128]{2,1,0:T(8,128)(2,1)S(1)} %copy-done.1, bf16[128,4,128,128]{3,2,1,0:T(8,128)(2,1)} %stiff_ref.1), custom_call_target="tpu_custom_call" | custom-call | tf_op jit(solution)/shard_map/products/pallas_call | solution.py:281
  67.4 0.4 fusion.1
  67.8 1.3 pad_maximum_fusion
  69.1 32.9 %exchange3.1 = f32[128,24,96]{2,1,0:T(8,128)} custom-call(f32[128,24,96]{2,1,0:T(8,128)} %bitcast.13), custom_call_target="tpu_custom_call" | custom-call | tf_op jit(solution)/shard_map/exchange3/pallas_call | solution.py:179
  102.0 1.8 copy.19
  103.8 0.0 copy-start.2
  103.8 0.0 copy-start.3
  103.8 0.8 reshape.44.part_ref
  104.6 0.0 copy-done.2
  104.6 0.0 copy-done.3
  104.6 17.1 %gathered_rows.1 = (s16[128,24,384]{2,1,0:T(8,128)(2,1)S(1)}, f32[128,1,128]{2,1,0:T(1,128)S(1)}) custom-call(s32[128,1,128]{2,1,0:T(1,128)S(1)} %copy-done.2, s32[64]{0:T(128)S(1)} %bitcast.12, f32[32,24,384]{2,1,0:T(8,128)S(1)} %reshape.44.part_ref), custom_call_target="tpu_custom_call" | custom-call | tf_op jit(solution)/shard_map/gathered_rows/pallas_call | solution.py:567
  121.7 57.9 %delivered.1 = f32[128,24,384]{2,1,0:T(8,128)S(1)} custom-call(s16[128,24,384]{2,1,0:T(8,128)(2,1)S(1)} %get-tuple-element.7.code_ref, f32[128,1,128]{2,1,0:T(1,128)S(1)} %get-tuple-element.8.scale_ref), custom_call_target="tpu_custom_call" | custom-call | tf_op jit(solution)/shard_map/delivered/pallas_call | solution.py:109
  179.7 2.2 %copy.21 = f32[128,24,384]{2,1,0:T(8,128)} copy(f32[128,24,384]{2,1,0:T(8,128)S(1)} %delivered.1) | data formatting | bytes 9437184
  (2 shorter events, 0.0 us)
Async XLA Ops:
  0.0 25.6 %copy-start = (bf16[64,24,128]{2,1,0:T(8,128)(2,1)S(1)}, bf16[64,24,128]{2,1,0:T(8,128)(2,1)}, u32[]{:S(2)}) copy-start(bf16[64,24,128]{2,1,0:T(8,128)(2,1)} %param.6) | copy-start | bytes 1179652
  48.5 1.1 copy-start.1
  103.8 0.8 copy-start.2
  103.8 0.8 copy-start.3
where the time goes:
time: 183 us; the launch traced here: 182 us
  Pallas kernels  167 us (91%)
  local copies, waits for them, and re-layouts  12.7 us (7%)
  other arithmetic  2.1 us (1%)
    pallas_call x3, Pallas kernels, exchange(): pl.pallas_call(functools.partial(exchange_kernel, gx, gy, count), out_sha...  74.2 us
    pallas_call x1, Pallas kernels, delivered(): pl.pallas_call(functools.partial(deliver_kernel, (gx, gy, cv)), out_shape...  57.9 us
    pallas_call x1, Pallas kernels, products(): pl.pallas_call(functools.partial(product_kernel, (cv, bps, group, per_ste...  17.7 us
    pallas_call x1, Pallas kernels, gathered_rows(): pl.pallas_call(functools.partial(gather_rows_kernel, (cv, bps, per_peer,...  17.1 us
    unnamed x10, local copies, waits for them, and re-layouts  4.15 us

commit v1 on v0

v1 whole, which is shorter than its diff:
```python
import functools

import jax
import jax.numpy as jnp
from jax import lax
from jax.experimental import pallas as pl
from jax.experimental.pallas import tpu as pltpu
from jax.sharding import PartitionSpec as P

MAXNB = 16
AXES = ("gx", "gy")
LANES = 128
SPAN = 32
ROUNDS = 16
WIDE = 8
TOP = 32767.0
MESH = pl.DeviceIdType.MESH
HBM = pl.BlockSpec(memory_space=pl.ANY)
VMEM = pl.BlockSpec(memory_space=pltpu.VMEM)
SMEM = pl.BlockSpec(memory_space=pltpu.SMEM)
NT = (((1,), (1,)), ((), ()))


def as_row(column):
    rows = column.shape[0]
    shape = (rows, LANES)
    eye = lax.broadcasted_iota(jnp.int32, shape, 0) == lax.broadcasted_iota(jnp.int32, shape, 1)
    return jnp.sum(jnp.where(eye, column, 0.0), axis=0, keepdims=True)


def as_column(row, rows):
    shape = (rows, LANES)
    eye = lax.broadcasted_iota(jnp.int32, shape, 0) == lax.broadcasted_iota(jnp.int32, shape, 1)
    return jnp.sum(jnp.where(eye, row, 0.0), axis=1, keepdims=True)


def coded(values):
    top = jnp.maximum(jnp.max(jnp.abs(values), axis=1, keepdims=True), 1e-30)
    code = jnp.round(values * (TOP / top)).astype(jnp.int32).astype(jnp.int16)
    return code, top * (1.0 / TOP)


def split(values):
    hi = values.astype(jnp.bfloat16)
    return hi, (values - hi.astype(jnp.float32)).astype(jnp.bfloat16)


def whole_kernel(
    slot_ref, owner_ref, meta_ref, prolong_ref, stiff_ref,
    out_ref,
    meta_in, req_ref, stage_ref, fetched_ref, mats_ref, pk_ref, cols_ref,
    code_ref, factor_ref, part_ref, scale_ref, spread_ref, total_ref,
    rows_ref, rows_scale, land_ref, land_scale, wide_ref,
    meta_send, meta_recv, fetch_send, fetch_recv, part_send, part_recv, fact_send, fact_recv,
    rows_send, rows_recv, rsc_send, rsc_recv, mats_sem, req_sem, out_sem,
):
    n, cv, dof = fetched_ref.shape
    bps = mats_ref.shape[1]
    width = out_ref.shape[2]
    gx, gy = lax.axis_index("gx"), lax.axis_index("gy")
    me = gx * 16 + gy
    z, core = gx // 2, lax.rem(gx, 2)
    x, y = gy // 4, lax.rem(gy, 4)
    to_gx = [lax.rem(z + j // 2, 4) * 2 + lax.rem(core + j, 2) for j in range(WIDE)]
    from_gx = [lax.rem(z + 4 - j // 2, 4) * 2 + lax.rem(core + j, 2) for j in range(WIDE)]

    def target(i, j):
        s = lax.rem(i * 5 + j * 3, 16)
        return to_gx[j], lax.rem(x + s // 4, 4) * 4 + lax.rem(y + s, 4)

    def source(i, j):
        s = lax.rem(i * 5 + j * 3, 16)
        return from_gx[j] * 16 + lax.rem(x + 4 - s // 4, 4) * 4 + lax.rem(y + 16 - s, 4)

    def each(fn):
        def body(i, c):
            for j in range(WIDE):
                fn(i, j)
            return c

        for j in range(1, WIDE):
            fn(0, j)
        lax.fori_loop(1, ROUNDS, body, 0)

    def remote(src, dst, send_sem, recv_sem, where):
        return pltpu.make_async_remote_copy(
            src_ref=src, dst_ref=dst, send_sem=send_sem, recv_sem=recv_sem,
            device_id=where, device_id_type=MESH,
        )

    def bulk(src, dst, send_sem, recv_sem, count):
        return remote(
            src.at[pl.ds(0, count)], dst.at[pl.ds(0, count)], send_sem, recv_sem, (gx, gy)
        )

    loads = [
        pltpu.make_async_copy(
            stiff_ref.at[pl.ds(b * 16, 16)], mats_ref.at[pl.ds(b * 16, 16)], mats_sem.at[b]
        )
        for b in range(n // 16)
    ]
    for copy in loads:
        copy.start()

    barrier = pltpu.get_barrier_semaphore()

    def greet(i, j):
        pl.semaphore_signal(barrier, inc=1, device_id=target(i, j), device_id_type=MESH)

    each(greet)
    meta_in[me] = meta_ref[me]
    cols_ref[...] = jnp.zeros_like(cols_ref)
    pl.semaphore_wait(barrier, n - 1)

    def ask(i, j):
        where = target(i, j)
        remote(
            meta_ref.at[where[0] * 16 + where[1]], meta_in.at[me],
            meta_send.at[0], meta_recv.at[0], where,
        ).start()

    each(ask)
    bulk(meta_ref, meta_in, meta_send.at[0], meta_recv.at[0], n - 1).wait()
    to_scalars = pltpu.make_async_copy(meta_in, req_ref, req_sem.at[0])
    to_scalars.start()
    to_scalars.wait()

    def fill(p, c):
        stage_ref[p] = prolong_ref[req_ref[p, 0, 0]]
        return c

    lax.fori_loop(0, n, fill, 0, unroll=8)

    def answer(i, j):
        where = target(i, j)
        remote(
            stage_ref.at[where[0] * 16 + where[1]], fetched_ref.at[me],
            fetch_send.at[0], fetch_recv.at[i], where,
        ).start()

    each(answer)
    fetched_ref[me] = prolong_ref[req_ref[me, 0, 0]]
    for copy in loads:
        copy.wait()

    def left_product(t):
        rows = fetched_ref[t]
        for h in range(bps // 2):
            pair = jnp.concatenate([mats_ref[t, 2 * h], mats_ref[t, 2 * h + 1]], axis=1)
            prod = jnp.dot(rows, pair, preferred_element_type=jnp.float32)
            hi, lo = split(prod)
            for u in range(2):
                at = slice(u * dof, (u + 1) * dof)
                pk_ref[t, 2 * h + u, :, 0:dof] = hi[:, at]
                pk_ref[t, 2 * h + u, :, dof : 2 * dof] = lo[:, at]

    bulk(stage_ref, fetched_ref, fetch_send.at[0], fetch_recv.at[0], WIDE - 1).wait_recv()
    left_product(me)
    for j in range(1, WIDE):
        left_product(source(0, j))

    def take(i, c):
        bulk(stage_ref, fetched_ref, fetch_send.at[0], fetch_recv.at[i], WIDE).wait_recv()
        for j in range(WIDE):
            left_product(source(i, j))
        return c

    lax.fori_loop(1, ROUNDS, take, 0)

    lane = lax.broadcasted_iota(jnp.int32, (cv, LANES), 1)

    def right_product(t, u):
        for q in range(bps):
            block = fetched_ref[slot_ref[t, q]]
            cols_ref[u, SPAN * q : SPAN * q + cv, 0:dof] = block
            cols_ref[u, SPAN * q : SPAN * q + cv, dof : 2 * dof] = block
        cols = cols_ref[u]
        one = None
        for q in range(bps - 1, -1, -1):
            prod = lax.dot_general(pk_ref[t, q], cols, NT, preferred_element_type=jnp.float32)
            one = prod if one is None else jnp.where(lane < SPAN * (q + 1), prod, one)
        code, factor = coded(one)
        code_ref[t] = code
        factor_ref[t] = as_row(factor)

    def give(i, j):
        where = target(i, j)
        peer = where[0] * 16 + where[1]
        remote(
            factor_ref.at[peer], scale_ref.at[me], fact_send.at[0], fact_recv.at[0], where
        ).start()
        remote(
            code_ref.at[peer], part_ref.at[me], part_send.at[0], part_recv.at[0], where
        ).start()

    def index(i, j):
        where = target(i, j)
        return where[0] * 16 + where[1]

    for j in range(WIDE):
        right_product(index(0, j), j)

    def work(i, c):
        for j in range(WIDE):
            right_product(index(i, j), j)

        for j in range(WIDE):
            @pl.when((i > 1) | (j > 0))
            def _():
                give(i - 1, j)
        return c

    lax.fori_loop(1, ROUNDS, work, 0)
    for j in range(WIDE):
        give(ROUNDS - 1, j)
    part_ref[me] = code_ref[me]
    scale_ref[me] = factor_ref[me]

    row_lane = lax.broadcasted_iota(jnp.int32, (1, LANES), 1)

    def locate(d, row):
        return jnp.where(row_lane == d, owner_ref[req_ref[d, 0, 0]], row)

    place = lax.fori_loop(0, n, locate, jnp.zeros((1, LANES), jnp.int32), unroll=8)
    hot = jnp.where(
        lax.broadcasted_iota(jnp.int32, (n, LANES), 0) == place, 1.0, 0.0
    ).astype(jnp.bfloat16)
    hot = jnp.concatenate([hot, hot], axis=1)

    bulk(code_ref, part_ref, part_send.at[0], part_recv.at[0], n - 1).wait()
    bulk(factor_ref, scale_ref, fact_send.at[0], fact_recv.at[0], n - 1).wait()

    blocks = [(lane + LANES * k) // cv for k in range(width // LANES)]

    def spread(d, c):
        values = part_ref[d].astype(jnp.int32).astype(jnp.float32) * as_column(scale_ref[d], cv)
        tiles = [jnp.zeros((cv, LANES), jnp.float32)] * (width // LANES)
        for q in range(bps):
            pos = req_ref[d, 0, 1 + q]
            moved = pltpu.roll(values, lax.rem(pos * cv - SPAN * q + LANES, LANES), 1)
            tiles = [jnp.where(b == pos, moved, tile) for b, tile in zip(blocks, tiles)]
        for k, tile in enumerate(tiles):
            spread_ref[k, pl.ds(d * cv, cv), :] = tile
        return c

    lax.fori_loop(0, n, spread, 0, unroll=8)

    def combine(c, carry):
        at = pl.ds(c, n, stride=cv)
        whole = jnp.concatenate(
            [spread_ref[k, at, :] for k in range(width // LANES)], axis=1
        )
        total = jnp.dot(
            hot, jnp.concatenate(split(whole), axis=0), preferred_element_type=jnp.float32
        )
        for k in range(width // LANES):
            total_ref[k, at, :] = total[:, LANES * k : LANES * (k + 1)]
        return carry

    lax.fori_loop(0, cv, combine, 0)

    def encode(o):
        rows = jnp.concatenate(
            [total_ref[k, pl.ds(o * cv, cv), :] for k in range(width // LANES)], axis=1
        )
        code, factor = coded(rows)
        rows_ref[o] = code
        rows_scale[o] = as_row(factor)

    def deliver(i, j):
        where = target(i, j)
        peer = where[0] * 16 + where[1]
        remote(
            rows_scale.at[peer], land_scale.at[me], rsc_send.at[0], rsc_recv.at[i], where
        ).start()
        remote(
            rows_ref.at[peer], land_ref.at[me], rows_send.at[0], rows_recv.at[i], where
        ).start()

    for j in range(WIDE):
        encode(index(0, j))

    def emit(i, c):
        for j in range(WIDE):
            encode(index(i, j))
        for j in range(WIDE):
            @pl.when((i > 1) | (j > 0))
            def _():
                deliver(i - 1, j)
        return c

    lax.fori_loop(1, ROUNDS, emit, 0)
    for j in range(WIDE):
        deliver(ROUNDS - 1, j)

    def out_copy(p):
        return pltpu.make_async_copy(
            wide_ref.at[p], out_ref.at[p], out_sem.at[p]
        )

    def decode(code, scale, p):
        wide_ref[p] = code.astype(jnp.int32).astype(jnp.float32) * as_column(scale, cv)

    def arrived(i, count):
        bulk(rows_ref, land_ref, rows_send.at[0], rows_recv.at[i], count).wait_recv()
        bulk(rows_scale, land_scale, rsc_send.at[0], rsc_recv.at[i], count).wait_recv()

    decode(rows_ref[me], rows_scale[me], me)
    arrived(0, WIDE - 1)
    for j in range(1, WIDE):
        p = source(0, j)
        decode(land_ref[p], land_scale[p], p)
    for j in range(WIDE):
        out_copy(source(0, j)).start()

    def drain(i, c):
        arrived(i, WIDE)
        for j in range(WIDE):
            p = source(i, j)
            decode(land_ref[p], land_scale[p], p)
        for j in range(WIDE):
            out_copy(source(i, j)).start()
        return c

    lax.fori_loop(1, ROUNDS, drain, 0)
    bulk(stage_ref, fetched_ref, fetch_send.at[0], fetch_recv.at[0], n - 1).wait_send()
    bulk(rows_ref, land_ref, rows_send.at[0], rows_recv.at[0], n - 1).wait_send()
    bulk(rows_scale, land_scale, rsc_send.at[0], rsc_recv.at[0], n - 1).wait_send()

    def finish(p, c):
        out_copy(p).wait()
        return c

    lax.fori_loop(0, n, finish, 0)


def whole(col_slot, owners, meta, prolong, stiffness):
    slots, bps, dof, _ = stiffness.shape
    cv = prolong.shape[1]
    n = meta.shape[0]
    width = MAXNB * cv
    sem = pltpu.SemaphoreType.DMA
    bf16, f32, i16, i32 = jnp.bfloat16, jnp.float32, jnp.int16, jnp.int32
    return pl.pallas_call(
        whole_kernel,
        out_shape=jax.ShapeDtypeStruct((n, cv, width), f32),
        in_specs=[SMEM, SMEM, VMEM, VMEM, HBM],
        out_specs=HBM,
        scratch_shapes=[
            pltpu.VMEM(meta.shape, i32),
            pltpu.SMEM(meta.shape, i32),
            pltpu.VMEM((n, cv, dof), bf16),
            pltpu.VMEM((n, cv, dof), bf16),
            pltpu.VMEM(stiffness.shape, bf16),
            pltpu.VMEM((n, bps, cv, 2 * dof), bf16),
            pltpu.VMEM((WIDE, LANES, 2 * dof), bf16),
            pltpu.VMEM((n, cv, LANES), i16),
            pltpu.VMEM((n, 1, LANES), f32),
            pltpu.VMEM((n, cv, LANES), i16),
            pltpu.VMEM((n, 1, LANES), f32),
            pltpu.VMEM((width // LANES, n * cv, LANES), f32),
            pltpu.VMEM((width // LANES, n * cv, LANES), f32),
            pltpu.VMEM((n, cv, width), i16),
            pltpu.VMEM((n, 1, LANES), f32),
            pltpu.VMEM((n, cv, width), i16),
            pltpu.VMEM((n, 1, LANES), f32),
            pltpu.VMEM((n, cv, width), f32),
            sem((1,)), sem((1,)),
            sem((1,)), sem((ROUNDS,)),
            sem((1,)), sem((1,)),
            sem((1,)), sem((1,)),
            sem((1,)), sem((ROUNDS,)),
            sem((1,)), sem((ROUNDS,)),
            sem((n // 16,)), sem((1,)), sem((n,)),
        ],
        compiler_params=pltpu.CompilerParams(
            collective_id=1, has_side_effects=True, vmem_limit_bytes=60 << 20
        ),
        name="whole",
    )(col_slot, owners, meta, prolong, stiffness)


def per_device(prolong, stiffness, request, col_slot, col_pos, coarse_owner):
    slots, bps = col_slot.shape
    meta = jnp.concatenate([request[:, None], col_pos], axis=1)
    meta = jnp.pad(meta, ((0, 0), (0, LANES - 1 - bps)))[:, None, :]
    return whole(col_slot, coarse_owner[:, 0], meta, prolong, stiffness)


def solution(mesh):
    placed = (
        P(AXES, None, None),
        P(AXES, None, None, None),
        P(AXES),
        P(AXES, None),
        P(AXES, None),
        P(AXES, None),
    )
    return jax.shard_map(
        per_device, mesh=mesh, in_specs=placed, out_specs=P(AXES, None, None), check_vma=False
    )
```

time: 183 us -> 117 us (0.64)
  Pallas kernels: 167 us -> 109 us
  local copies, waits for them, and re-layouts: 12.7 us -> 6.98 us
    pallas_call x6 -> x1, Pallas kernels: 167 us -> 109 us  [whole(): pl.pallas_call(whole_kernel, out_shape=jax.ShapeDtypeStruct((n, cv, width...]
    slice x2 -> x0, local copies, waits for them, and re-layouts: 3.65 us -> none  [the longest x1 3.28 us: per_device(): meta_in[:, 0, :per_peer].reshape(-1)]
    reshape x2 -> x0, local copies, waits for them, and re-layouts: 2.59 us -> none  [the longest x1 1.81 us: per_device(): flat.reshape(slots // group, group, cv, bps * cv).transpose(0, 2, 1, 3)]
    unnamed x10 -> x2, local copies, waits for them, and re-layouts: 4.15 us -> 6.24 us
where the time goes in v1:
time: 117 us
  Pallas kernels  109 us (93%)
  local copies, waits for them, and re-layouts  6.98 us (6%)
    pallas_call x1, Pallas kernels, whole(): pl.pallas_call(whole_kernel, out_shape=jax.ShapeDtypeStruct((n, cv, width...  109 us
    unnamed x2, local copies, waits for them, and re-layouts  6.24 us

profile of v1, /device:TPU:1, one launch (start us, length us, event | category | flops | bytes accessed | tf_op | source)
XLA Modules:
  0.0 117.0 jit_solution(6824418068891728561)
XLA Ops:
  0.0 0.7 pad_add_fusion
  0.7 0.1 copy.10
  0.8 0.6 pad.4
  1.4 1.4 %copy.11.slot_ref = s32[128,4]{1,0:T(8,128)} copy(s32[128,4]{0,1:T(4,128)} %param.9) | data formatting | bytes 4096 | tf_op args[3]
  2.8 109.4 %whole.1 = f32[128,24,384]{2,1,0:T(8,128)} custom-call(s32[128,4]{1,0:T(8,128)} %copy.11.slot_ref, s32[64]{0:T(128)} %bitcast.4, s32[128,1,128]{2,1,0:T(1,128)} %bitcast.3, bf16[64,24,128]{2,1,0:T(8,128)(2,1)} %prolong_ref.1, bf16[128,4,128,128]{3,2,1,0:T(8,128)(2,1)} %stiff_ref.1), custom_call_target="tpu_custom_call" | custom-call | tf_op jit(solution)/shard_map/whole/pallas_call | solution.py:344
  112.2 4.8 %copy.13 = f32[128,24,384]{2,1,0:T(8,128)} copy(f32[128,24,384]{2,1,0:T(8,128)} %whole.1) | data formatting | bytes 9437184

commit v2 on v1

--- a/solution.py
+++ b/solution.py
@@ -46,13 +46,13 @@
 
 
 def whole_kernel(
-    slot_ref, owner_ref, meta_ref, prolong_ref, stiff_ref,
+    slot_ref, pos_ref, ask_ref, owner_ref, prolong_ref, stiff_ref,
     out_ref,
-    meta_in, req_ref, stage_ref, fetched_ref, mats_ref, pk_ref, cols_ref,
+    meta_ref, mid_ref, meta_in, req_ref, stage_ref, fetched_ref, mats_ref, pk_ref, cols_ref,
     code_ref, factor_ref, part_ref, scale_ref, spread_ref, total_ref,
-    rows_ref, rows_scale, land_ref, land_scale, wide_ref,
-    meta_send, meta_recv, fetch_send, fetch_recv, part_send, part_recv, fact_send, fact_recv,
-    rows_send, rows_recv, rsc_send, rsc_recv, mats_sem, req_sem, out_sem,
+    rows_ref, rows_scale, land_ref, land_scale,
+    near_send, near_recv, far_send, far_recv, fetch_send, fetch_recv, part_send, part_recv, fact_send, fact_recv,
+    rows_send, rows_recv, rsc_send, rsc_recv, mats_sem, req_sem,
 ):
     n, cv, dof = fetched_ref.shape
     bps = mats_ref.shape[1]
@@ -103,30 +103,49 @@
         copy.start()
 
     barrier = pltpu.get_barrier_semaphore()
-
-    def greet(i, j):
-        pl.semaphore_signal(barrier, inc=1, device_id=target(i, j), device_id_type=MESH)
-
-    each(greet)
-    meta_in[me] = meta_ref[me]
+    near = [(g, gy) for g in to_gx[1:]]
+    far = [(gx, lax.rem(x + s // 4, 4) * 4 + lax.rem(y + s, 4)) for s in range(1, 16)]
+    for where in near + far:
+        pl.semaphore_signal(barrier, inc=1, device_id=where, device_id_type=MESH)
+
+    row_lane = lax.broadcasted_iota(jnp.int32, (1, LANES), 1)
+
+    def describe(h, c):
+        for g in range(8):
+            p = g * 16 + h
+            row = jnp.where(row_lane == 0, ask_ref[p], 0)
+            for q in range(bps):
+                row = jnp.where(row_lane == 1 + q, pos_ref[q, p], row)
+            meta_ref[g, h] = row
+        return c
+
+    lax.fori_loop(0, 16, describe, 0)
+    mid_ref[gx] = meta_ref[gx]
     cols_ref[...] = jnp.zeros_like(cols_ref)
-    pl.semaphore_wait(barrier, n - 1)
-
-    def ask(i, j):
-        where = target(i, j)
-        remote(
-            meta_ref.at[where[0] * 16 + where[1]], meta_in.at[me],
-            meta_send.at[0], meta_recv.at[0], where,
-        ).start()
-
-    each(ask)
-    bulk(meta_ref, meta_in, meta_send.at[0], meta_recv.at[0], n - 1).wait()
+    pl.semaphore_wait(barrier, 22)
+    for where in near:
+        remote(
+            meta_ref.at[where[0]], mid_ref.at[gx], near_send.at[0], near_recv.at[0], where
+        ).start()
+    bulk(meta_ref, mid_ref, near_send.at[0], near_recv.at[0], 7).wait()
+    for where in far:
+        remote(
+            mid_ref.at[:, where[1]], meta_in.at[:, gy], far_send.at[0], far_recv.at[0], where
+        ).start()
+    meta_in[:, gy] = mid_ref[:, gy]
+    remote(
+        mid_ref.at[:, pl.ds(0, 15)], meta_in.at[:, pl.ds(0, 15)],
+        far_send.at[0], far_recv.at[0], (gx, gy),
+    ).wait()
     to_scalars = pltpu.make_async_copy(meta_in, req_ref, req_sem.at[0])
     to_scalars.start()
     to_scalars.wait()
 
+    def asked(d, k):
+        return req_ref[d // 16, lax.rem(d, 16), 0, k]
+
     def fill(p, c):
-        stage_ref[p] = prolong_ref[req_ref[p, 0, 0]]
+        stage_ref[p] = prolong_ref[asked(p, 0)]
         return c
 
     lax.fori_loop(0, n, fill, 0, unroll=8)
@@ -139,20 +158,20 @@
         ).start()
 
     each(answer)
-    fetched_ref[me] = prolong_ref[req_ref[me, 0, 0]]
+    fetched_ref[me] = prolong_ref[asked(me, 0)]
     for copy in loads:
         copy.wait()
 
     def left_product(t):
         rows = fetched_ref[t]
+        parts = []
         for h in range(bps // 2):
             pair = jnp.concatenate([mats_ref[t, 2 * h], mats_ref[t, 2 * h + 1]], axis=1)
             prod = jnp.dot(rows, pair, preferred_element_type=jnp.float32)
-            hi, lo = split(prod)
-            for u in range(2):
-                at = slice(u * dof, (u + 1) * dof)
-                pk_ref[t, 2 * h + u, :, 0:dof] = hi[:, at]
-                pk_ref[t, 2 * h + u, :, dof : 2 * dof] = lo[:, at]
+            parts += [prod[:, 0:dof], prod[:, dof : 2 * dof]]
+        hi, lo = split(jnp.concatenate(parts, axis=0))
+        pk_ref[t, :, 0:dof] = hi
+        pk_ref[t, :, dof : 2 * dof] = lo
 
     bulk(stage_ref, fetched_ref, fetch_send.at[0], fetch_recv.at[0], WIDE - 1).wait_recv()
     left_product(me)
@@ -171,14 +190,13 @@
 
     def right_product(t, u):
         for q in range(bps):
-            block = fetched_ref[slot_ref[t, q]]
+            block = fetched_ref[slot_ref[q, t]]
             cols_ref[u, SPAN * q : SPAN * q + cv, 0:dof] = block
             cols_ref[u, SPAN * q : SPAN * q + cv, dof : 2 * dof] = block
-        cols = cols_ref[u]
-        one = None
-        for q in range(bps - 1, -1, -1):
-            prod = lax.dot_general(pk_ref[t, q], cols, NT, preferred_element_type=jnp.float32)
-            one = prod if one is None else jnp.where(lane < SPAN * (q + 1), prod, one)
+        prod = lax.dot_general(pk_ref[t], cols_ref[u], NT, preferred_element_type=jnp.float32)
+        one = prod[(bps - 1) * cv :]
+        for q in range(bps - 2, -1, -1):
+            one = jnp.where(lane < SPAN * (q + 1), prod[q * cv : (q + 1) * cv], one)
         code, factor = coded(one)
         code_ref[t] = code
         factor_ref[t] = as_row(factor)
@@ -216,10 +234,8 @@
     part_ref[me] = code_ref[me]
     scale_ref[me] = factor_ref[me]
 
-    row_lane = lax.broadcasted_iota(jnp.int32, (1, LANES), 1)
-
     def locate(d, row):
-        return jnp.where(row_lane == d, owner_ref[req_ref[d, 0, 0]], row)
+        return jnp.where(row_lane == d, owner_ref[asked(d, 0)], row)
 
     place = lax.fori_loop(0, n, locate, jnp.zeros((1, LANES), jnp.int32), unroll=8)
     hot = jnp.where(
@@ -236,7 +252,7 @@
         values = part_ref[d].astype(jnp.int32).astype(jnp.float32) * as_column(scale_ref[d], cv)
         tiles = [jnp.zeros((cv, LANES), jnp.float32)] * (width // LANES)
         for q in range(bps):
-            pos = req_ref[d, 0, 1 + q]
+            pos = asked(d, 1 + q)
             moved = pltpu.roll(values, lax.rem(pos * cv - SPAN * q + LANES, LANES), 1)
             tiles = [jnp.where(b == pos, moved, tile) for b, tile in zip(blocks, tiles)]
         for k, tile in enumerate(tiles):
@@ -293,13 +309,8 @@
     for j in range(WIDE):
         deliver(ROUNDS - 1, j)
 
-    def out_copy(p):
-        return pltpu.make_async_copy(
-            wide_ref.at[p], out_ref.at[p], out_sem.at[p]
-        )
-
     def decode(code, scale, p):
-        wide_ref[p] = code.astype(jnp.int32).astype(jnp.float32) * as_column(scale, cv)
+        out_ref[p] = code.astype(jnp.int32).astype(jnp.float32) * as_column(scale, cv)
 
     def arrived(i, count):
         bulk(rows_ref, land_ref, rows_send.at[0], rows_recv.at[i], count).wait_recv()
@@ -310,16 +321,12 @@
     for j in range(1, WIDE):
         p = source(0, j)
         decode(land_ref[p], land_scale[p], p)
-    for j in range(WIDE):
-        out_copy(source(0, j)).start()
 
     def drain(i, c):
         arrived(i, WIDE)
         for j in range(WIDE):
             p = source(i, j)
             decode(land_ref[p], land_scale[p], p)
-        for j in range(WIDE):
-            out_copy(source(i, j)).start()
         return c
 
     lax.fori_loop(1, ROUNDS, drain, 0)
@@ -327,32 +334,28 @@
     bulk(rows_ref, land_ref, rows_send.at[0], rows_recv.at[0], n - 1).wait_send()
     bulk(rows_scale, land_scale, rsc_send.at[0], rsc_recv.at[0], n - 1).wait_send()
 
-    def finish(p, c):
-        out_copy(p).wait()
-        return c
-
-    lax.fori_loop(0, n, finish, 0)
-
-
-def whole(col_slot, owners, meta, prolong, stiffness):
+
+def whole(col_slot, col_pos, request, owners, prolong, stiffness):
     slots, bps, dof, _ = stiffness.shape
     cv = prolong.shape[1]
-    n = meta.shape[0]
+    n = slots
     width = MAXNB * cv
     sem = pltpu.SemaphoreType.DMA
     bf16, f32, i16, i32 = jnp.bfloat16, jnp.float32, jnp.int16, jnp.int32
     return pl.pallas_call(
         whole_kernel,
         out_shape=jax.ShapeDtypeStruct((n, cv, width), f32),
-        in_specs=[SMEM, SMEM, VMEM, VMEM, HBM],
-        out_specs=HBM,
+        in_specs=[SMEM, SMEM, SMEM, SMEM, VMEM, HBM],
+        out_specs=VMEM,
         scratch_shapes=[
-            pltpu.VMEM(meta.shape, i32),
-            pltpu.SMEM(meta.shape, i32),
+            pltpu.VMEM((8, 16, 1, LANES), i32),
+            pltpu.VMEM((8, 16, 1, LANES), i32),
+            pltpu.VMEM((8, 16, 1, LANES), i32),
+            pltpu.SMEM((8, 16, 1, LANES), i32),
             pltpu.VMEM((n, cv, dof), bf16),
             pltpu.VMEM((n, cv, dof), bf16),
             pltpu.VMEM(stiffness.shape, bf16),
-            pltpu.VMEM((n, bps, cv, 2 * dof), bf16),
+            pltpu.VMEM((n, bps * cv, 2 * dof), bf16),
             pltpu.VMEM((WIDE, LANES, 2 * dof), bf16),
             pltpu.VMEM((n, cv, LANES), i16),
             pltpu.VMEM((n, 1, LANES), f32),
@@ -364,27 +367,24 @@
             pltpu.VMEM((n, 1, LANES), f32),
             pltpu.VMEM((n, cv, width), i16),
             pltpu.VMEM((n, 1, LANES), f32),
-            pltpu.VMEM((n, cv, width), f32),
+            sem((1,)), sem((1,)),
             sem((1,)), sem((1,)),
             sem((1,)), sem((ROUNDS,)),
             sem((1,)), sem((1,)),
             sem((1,)), sem((1,)),
             sem((1,)), sem((ROUNDS,)),
             sem((1,)), sem((ROUNDS,)),
-            sem((n // 16,)), sem((1,)), sem((n,)),
+            sem((n // 16,)), sem((1,)),
         ],
         compiler_params=pltpu.CompilerParams(
-            collective_id=1, has_side_effects=True, vmem_limit_bytes=60 << 20
+            collective_id=1, has_side_effects=True, vmem_limit_bytes=50 << 20
         ),
         name="whole",
-    )(col_slot, owners, meta, prolong, stiffness)
+    )(col_slot, col_pos, request, owners, prolong, stiffness)
 
 
 def per_device(prolong, stiffness, request, col_slot, col_pos, coarse_owner):
-    slots, bps = col_slot.shape
-    meta = jnp.concatenate([request[:, None], col_pos], axis=1)
-    meta = jnp.pad(meta, ((0, 0), (0, LANES - 1 - bps)))[:, None, :]
-    return whole(col_slot, coarse_owner[:, 0], meta, prolong, stiffness)
+    return whole(col_slot.T, col_pos.T, request, coarse_owner[:, 0], prolong, stiffness)
 
 
 def solution(mesh):

time: 117 us -> 107 us (0.915)
  Pallas kernels: 109 us -> 98 us
  local copies, waits for them, and re-layouts: 6.98 us -> 8.49 us
    pallas_call x1, Pallas kernels: 109 us -> 98 us  [whole(): pl.pallas_call(whole_kernel, out_shape=jax.ShapeDtypeStruct((n, cv, width...]
    unnamed x2 -> x11, local copies, waits for them, and re-layouts: 6.24 us -> 8.49 us
where the time goes in v2:
time: 107 us
  Pallas kernels  98 us (92%)
  local copies, waits for them, and re-layouts  8.49 us (8%)
    pallas_call x1, Pallas kernels, whole(): pl.pallas_call(whole_kernel, out_shape=jax.ShapeDtypeStruct((n, cv, width...  98 us
    unnamed x11, local copies, waits for them, and re-layouts  8.49 us

profile of v2, /device:TPU:1, one launch (start us, length us, event | category | flops | bytes accessed | tf_op | source)
XLA Modules:
  0.0 106.5 jit_solution(11497240849182821293)
XLA Ops:
  0.0 0.0 copy-start
  0.0 1.0 copy-done
  1.0 0.0 copy-start.1
  1.0 0.7 copy-done.1
  1.7 0.0 copy-start.2
  1.7 0.7 copy-done.2
  2.4 0.0 copy-start.3
  2.4 0.7 copy-done.3
  3.0 0.0 copy-start.4
  3.0 0.7 copy-done.4
  3.7 98.0 %whole.1 = f32[128,24,384]{2,1,0:T(8,128)} custom-call(s32[4,128]{1,0:T(4,128)S(1)} %bitcast.3, s32[4,128]{1,0:T(4,128)S(1)} %bitcast.4, s32[128]{0:T(128)S(1)} %copy-done.3, s32[64]{0:T(128)S(1)} %bitcast.5, bf16[64,24,128]{2,1,0:T(8,128)(2,1)S(1)} %copy-done, bf16[128,4,128,128]{3,2,1,0:T(8,128)(2,1)} %stiff_ref.1), custom_call_target="tpu_custom_call" | custom-call | tf_op jit(solution)/shard_map/whole/pallas_call | solution.py:345
  101.7 4.8 %copy.8 = f32[128,24,384]{2,1,0:T(8,128)} copy(f32[128,24,384]{2,1,0:T(8,128)} %whole.1) | data formatting | bytes 9437184
Async XLA Ops:
  0.0 1.0 copy-start
  1.0 0.7 copy-start.1
  1.7 0.7 copy-start.2
  2.4 0.7 copy-start.3
  3.0 0.7 copy-start.4

commit v3 on v2

--- a/solution.py
+++ b/solution.py
@@ -11,32 +11,37 @@
 AXES = ("gx", "gy")
 LANES = 128
 SPAN = 32
+CHUNKS = ((0, 8), (8, 16))
 ROUNDS = 16
 WIDE = 8
 TOP = 32767.0
 MESH = pl.DeviceIdType.MESH
-HBM = pl.BlockSpec(memory_space=pl.ANY)
+HBM = pl.BlockSpec(memory_space=pltpu.HBM)
 VMEM = pl.BlockSpec(memory_space=pltpu.VMEM)
-SMEM = pl.BlockSpec(memory_space=pltpu.SMEM)
 NT = (((1,), (1,)), ((), ()))
 
 
-def as_row(column):
-    rows = column.shape[0]
+def diagonal(rows, first):
     shape = (rows, LANES)
-    eye = lax.broadcasted_iota(jnp.int32, shape, 0) == lax.broadcasted_iota(jnp.int32, shape, 1)
-    return jnp.sum(jnp.where(eye, column, 0.0), axis=0, keepdims=True)
-
-
-def as_column(row, rows):
-    shape = (rows, LANES)
-    eye = lax.broadcasted_iota(jnp.int32, shape, 0) == lax.broadcasted_iota(jnp.int32, shape, 1)
-    return jnp.sum(jnp.where(eye, row, 0.0), axis=1, keepdims=True)
+    return (
+        lax.broadcasted_iota(jnp.int32, shape, 0) + first
+        == lax.broadcasted_iota(jnp.int32, shape, 1)
+    )
+
+
+def as_row(column, first=0):
+    return jnp.sum(
+        jnp.where(diagonal(column.shape[0], first), column, 0.0), axis=0, keepdims=True
+    )
+
+
+def as_column(row, rows, first=0):
+    return jnp.sum(jnp.where(diagonal(rows, first), row, 0.0), axis=1, keepdims=True)
 
 
 def coded(values):
     top = jnp.maximum(jnp.max(jnp.abs(values), axis=1, keepdims=True), 1e-30)
-    code = jnp.round(values * (TOP / top)).astype(jnp.int32).astype(jnp.int16)
+    code = jnp.round(values * (TOP / top)).astype(jnp.int32)
     return code, top * (1.0 / TOP)
 
 
@@ -46,13 +51,14 @@
 
 
 def whole_kernel(
-    slot_ref, pos_ref, ask_ref, owner_ref, prolong_ref, stiff_ref,
+    slot_in, pos_in, ask_in, owner_in, prolong_in, stiff_ref,
     out_ref,
+    slot_ref, pos_ref, ask_ref, owner_ref, prolong_ref,
     meta_ref, mid_ref, meta_in, req_ref, stage_ref, fetched_ref, mats_ref, pk_ref, cols_ref,
-    code_ref, factor_ref, part_ref, scale_ref, spread_ref, total_ref,
-    rows_ref, rows_scale, land_ref, land_scale,
+    code_a, code_b, factor_ref, part_a, part_b, scale_ref, table_ref, spread_ref, total_ref,
+    rows_a, rows_b, rows_scale, land_a, land_b, land_scale,
     near_send, near_recv, far_send, far_recv, fetch_send, fetch_recv, part_send, part_recv, fact_send, fact_recv,
-    rows_send, rows_recv, rsc_send, rsc_recv, mats_sem, req_sem,
+    rows_send, rows_recv, rsc_send, rsc_recv, mats_sem, req_sem, arg_sem,
 ):
     n, cv, dof = fetched_ref.shape
     bps = mats_ref.shape[1]
@@ -93,6 +99,17 @@
             src.at[pl.ds(0, count)], dst.at[pl.ds(0, count)], send_sem, recv_sem, (gx, gy)
         )
 
+    small = [
+        pltpu.make_async_copy(src, dst, arg_sem.at[k])
+        for k, (src, dst) in enumerate(
+            (
+                (ask_in, ask_ref), (pos_in, pos_ref), (slot_in, slot_ref),
+                (owner_in, owner_ref), (prolong_in, prolong_ref),
+            )
+        )
+    ]
+    for copy in small:
+        copy.start()
     loads = [
         pltpu.make_async_copy(
             stiff_ref.at[pl.ds(b * 16, 16)], mats_ref.at[pl.ds(b * 16, 16)], mats_sem.at[b]
@@ -119,9 +136,16 @@
             meta_ref[g, h] = row
         return c
 
+    for copy in small[:2]:
+        copy.wait()
     lax.fori_loop(0, 16, describe, 0)
     mid_ref[gx] = meta_ref[gx]
     cols_ref[...] = jnp.zeros_like(cols_ref)
+    unit_row = lax.broadcasted_iota(jnp.int32, (SPAN, width), 0)
+    unit_col = lax.broadcasted_iota(jnp.int32, (SPAN, width), 1)
+    for k in range(MAXNB):
+        unit = (unit_row < cv) & (unit_col == unit_row + cv * k)
+        table_ref[k] = jnp.where(unit, 1.0, 0.0).astype(jnp.bfloat16)
     pl.semaphore_wait(barrier, 22)
     for where in near:
         remote(
@@ -137,6 +161,8 @@
         mid_ref.at[:, pl.ds(0, 15)], meta_in.at[:, pl.ds(0, 15)],
         far_send.at[0], far_recv.at[0], (gx, gy),
     ).wait()
+    for copy in small[2:]:
+        copy.wait()
     to_scalars = pltpu.make_async_copy(meta_in, req_ref, req_sem.at[0])
     to_scalars.start()
     to_scalars.wait()
@@ -198,7 +224,8 @@
         for q in range(bps - 2, -1, -1):
             one = jnp.where(lane < SPAN * (q + 1), prod[q * cv : (q + 1) * cv], one)
         code, factor = coded(one)
-        code_ref[t] = code
+        for (first, rows), ref in zip(CHUNKS, (code_a, code_b)):
+            ref[t] = code[first : first + rows].astype(jnp.int16)
         factor_ref[t] = as_row(factor)
 
     def give(i, j):
@@ -208,7 +235,14 @@
             factor_ref.at[peer], scale_ref.at[me], fact_send.at[0], fact_recv.at[0], where
         ).start()
         remote(
-            code_ref.at[peer], part_ref.at[me], part_send.at[0], part_recv.at[0], where
+            code_a.at[peer], part_a.at[me], part_send.at[0], part_recv.at[0], where
+        ).start()
+
+    def give_rest(i, j):
+        where = target(i, j)
+        remote(
+            code_b.at[where[0] * 16 + where[1]], part_b.at[me],
+            part_send.at[1], part_recv.at[1], where,
         ).start()
 
     def index(i, j):
@@ -231,7 +265,9 @@
     lax.fori_loop(1, ROUNDS, work, 0)
     for j in range(WIDE):
         give(ROUNDS - 1, j)
-    part_ref[me] = code_ref[me]
+    each(give_rest)
+    part_a[me] = code_a[me]
+    part_b[me] = code_b[me]
     scale_ref[me] = factor_ref[me]
 
     def locate(d, row):
@@ -243,96 +279,115 @@
     ).astype(jnp.bfloat16)
     hot = jnp.concatenate([hot, hot], axis=1)
 
-    bulk(code_ref, part_ref, part_send.at[0], part_recv.at[0], n - 1).wait()
-    bulk(factor_ref, scale_ref, fact_send.at[0], fact_recv.at[0], n - 1).wait()
-
-    blocks = [(lane + LANES * k) // cv for k in range(width // LANES)]
-
-    def spread(d, c):
-        values = part_ref[d].astype(jnp.int32).astype(jnp.float32) * as_column(scale_ref[d], cv)
-        tiles = [jnp.zeros((cv, LANES), jnp.float32)] * (width // LANES)
-        for q in range(bps):
-            pos = asked(d, 1 + q)
-            moved = pltpu.roll(values, lax.rem(pos * cv - SPAN * q + LANES, LANES), 1)
-            tiles = [jnp.where(b == pos, moved, tile) for b, tile in zip(blocks, tiles)]
-        for k, tile in enumerate(tiles):
-            spread_ref[k, pl.ds(d * cv, cv), :] = tile
-        return c
-
-    lax.fori_loop(0, n, spread, 0, unroll=8)
+    tiles = width // LANES
+
+    def spread(part, first, rows, d):
+        values = part[d].astype(jnp.int32).astype(jnp.float32)
+        values = values * as_column(scale_ref[d], rows, first)
+        hi = values.astype(jnp.bfloat16).astype(jnp.float32)
+        both = jnp.concatenate([hi, values - hi], axis=0).astype(jnp.bfloat16)
+        units = jnp.concatenate(
+            [table_ref[asked(d, 1 + q)] for q in range(bps)], axis=0
+        )
+        moved = jnp.dot(both, units, preferred_element_type=jnp.float32)
+        moved = moved[:rows] + moved[rows:]
+        for k in range(tiles):
+            spread_ref[k, pl.ds(d * cv + first, rows), :] = moved[:, LANES * k : LANES * (k + 1)]
 
     def combine(c, carry):
         at = pl.ds(c, n, stride=cv)
-        whole = jnp.concatenate(
-            [spread_ref[k, at, :] for k in range(width // LANES)], axis=1
-        )
+        every = jnp.concatenate([spread_ref[k, at, :] for k in range(tiles)], axis=1)
         total = jnp.dot(
-            hot, jnp.concatenate(split(whole), axis=0), preferred_element_type=jnp.float32
-        )
-        for k in range(width // LANES):
+            hot, jnp.concatenate(split(every), axis=0), preferred_element_type=jnp.float32
+        )
+        for k in range(tiles):
             total_ref[k, at, :] = total[:, LANES * k : LANES * (k + 1)]
         return carry
 
-    lax.fori_loop(0, cv, combine, 0)
-
-    def encode(o):
-        rows = jnp.concatenate(
-            [total_ref[k, pl.ds(o * cv, cv), :] for k in range(width // LANES)], axis=1
-        )
-        code, factor = coded(rows)
-        rows_ref[o] = code
-        rows_scale[o] = as_row(factor)
-
-    def deliver(i, j):
-        where = target(i, j)
-        peer = where[0] * 16 + where[1]
-        remote(
-            rows_scale.at[peer], land_scale.at[me], rsc_send.at[0], rsc_recv.at[i], where
-        ).start()
-        remote(
-            rows_ref.at[peer], land_ref.at[me], rows_send.at[0], rows_recv.at[i], where
-        ).start()
-
-    for j in range(WIDE):
-        encode(index(0, j))
-
-    def emit(i, c):
+    for h, ((first, rows), code_ref, part, rows_ref, land_ref) in enumerate(
+        zip(CHUNKS, (code_a, code_b), (part_a, part_b), (rows_a, rows_b), (land_a, land_b))
+    ):
+        bulk(code_ref, part, part_send.at[h], part_recv.at[h], n - 1).wait()
+        if h == 0:
+            bulk(factor_ref, scale_ref, fact_send.at[0], fact_recv.at[0], n - 1).wait()
+
+        def spread_some(i, c):
+            for j in range(WIDE):
+                spread(part, first, rows, i * WIDE + j)
+            return c
+
+        lax.fori_loop(0, ROUNDS, spread_some, 0)
+        lax.fori_loop(first, first + rows, combine, 0)
+
+        def encode(o):
+            row = jnp.concatenate(
+                [total_ref[k, pl.ds(o * cv + first, rows), :] for k in range(tiles)], axis=1
+            )
+            code, factor = coded(row)
+            rows_ref[o] = code.astype(jnp.int16)
+            rows_scale[h, o] = as_row(factor, first)
+
+        def deliver(i, j):
+            where = target(i, j)
+            peer = where[0] * 16 + where[1]
+            remote(
+                rows_scale.at[h, peer], land_scale.at[h, me],
+                rsc_send.at[h], rsc_recv.at[h, i], where,
+            ).start()
+            remote(
+                rows_ref.at[peer], land_ref.at[me],
+                rows_send.at[h], rows_recv.at[h, i], where,
+            ).start()
+
         for j in range(WIDE):
-            encode(index(i, j))
+            encode(index(0, j))
+
+        def emit(i, c):
+            for j in range(WIDE):
+                encode(index(i, j))
+            for j in range(WIDE):
+                @pl.when((i > 1) | (j > 0))
+                def _():
+                    deliver(i - 1, j)
+            return c
+
+        lax.fori_loop(1, ROUNDS, emit, 0)
         for j in range(WIDE):
-            @pl.when((i > 1) | (j > 0))
-            def _():
-                deliver(i - 1, j)
-        return c
-
-    lax.fori_loop(1, ROUNDS, emit, 0)
-    for j in range(WIDE):
-        deliver(ROUNDS - 1, j)
-
-    def decode(code, scale, p):
-        out_ref[p] = code.astype(jnp.int32).astype(jnp.float32) * as_column(scale, cv)
-
-    def arrived(i, count):
-        bulk(rows_ref, land_ref, rows_send.at[0], rows_recv.at[i], count).wait_recv()
-        bulk(rows_scale, land_scale, rsc_send.at[0], rsc_recv.at[i], count).wait_recv()
-
-    decode(rows_ref[me], rows_scale[me], me)
-    arrived(0, WIDE - 1)
-    for j in range(1, WIDE):
-        p = source(0, j)
-        decode(land_ref[p], land_scale[p], p)
-
-    def drain(i, c):
-        arrived(i, WIDE)
-        for j in range(WIDE):
-            p = source(i, j)
-            decode(land_ref[p], land_scale[p], p)
-        return c
-
-    lax.fori_loop(1, ROUNDS, drain, 0)
+            deliver(ROUNDS - 1, j)
+
+    for h, ((first, rows), rows_ref, land_ref) in enumerate(
+        zip(CHUNKS, (rows_a, rows_b), (land_a, land_b))
+    ):
+        def decode(code, scale, p):
+            out_ref[p, first : first + rows, :] = code.astype(jnp.int32).astype(
+                jnp.float32
+            ) * as_column(scale, rows, first)
+
+        def arrived(i, count):
+            bulk(rows_ref, land_ref, rows_send.at[h], rows_recv.at[h, i], count).wait_recv()
+            bulk(
+                rows_scale.at[h], land_scale.at[h], rsc_send.at[h], rsc_recv.at[h, i], count
+            ).wait_recv()
+
+        decode(rows_ref[me], rows_scale[h, me], me)
+        arrived(0, WIDE - 1)
+        for j in range(1, WIDE):
+            p = source(0, j)
+            decode(land_ref[p], land_scale[h, p], p)
+
+        def drain(i, c):
+            arrived(i, WIDE)
+            for j in range(WIDE):
+                p = source(i, j)
+                decode(land_ref[p], land_scale[h, p], p)
+            return c
+
+        lax.fori_loop(1, ROUNDS, drain, 0)
+        bulk(rows_ref, land_ref, rows_send.at[h], rows_recv.at[h, 0], n - 1).wait_send()
+        bulk(
+            rows_scale.at[h], land_scale.at[h], rsc_send.at[h], rsc_recv.at[h, 0], n - 1
+        ).wait_send()
     bulk(stage_ref, fetched_ref, fetch_send.at[0], fetch_recv.at[0], n - 1).wait_send()
-    bulk(rows_ref, land_ref, rows_send.at[0], rows_recv.at[0], n - 1).wait_send()
-    bulk(rows_scale, land_scale, rsc_send.at[0], rsc_recv.at[0], n - 1).wait_send()
 
 
 def whole(col_slot, col_pos, request, owners, prolong, stiffness):
@@ -345,9 +400,14 @@
     return pl.pallas_call(
         whole_kernel,
         out_shape=jax.ShapeDtypeStruct((n, cv, width), f32),
-        in_specs=[SMEM, SMEM, SMEM, SMEM, VMEM, HBM],
+        in_specs=[HBM] * 6,
         out_specs=VMEM,
         scratch_shapes=[
+            pltpu.SMEM(col_slot.shape, i32),
+            pltpu.SMEM(col_pos.shape, i32),
+            pltpu.SMEM(request.shape, i32),
+            pltpu.SMEM(owners.shape, i32),
+            pltpu.VMEM(prolong.shape, bf16),
             pltpu.VMEM((8, 16, 1, LANES), i32),
             pltpu.VMEM((8, 16, 1, LANES), i32),
             pltpu.VMEM((8, 16, 1, LANES), i32),
@@ -357,27 +417,28 @@
             pltpu.VMEM(stiffness.shape, bf16),
             pltpu.VMEM((n, bps * cv, 2 * dof), bf16),
             pltpu.VMEM((WIDE, LANES, 2 * dof), bf16),
-            pltpu.VMEM((n, cv, LANES), i16),
+            *[pltpu.VMEM((n, rows, LANES), i16) for _, rows in CHUNKS],
             pltpu.VMEM((n, 1, LANES), f32),
-            pltpu.VMEM((n, cv, LANES), i16),
+            *[pltpu.VMEM((n, rows, LANES), i16) for _, rows in CHUNKS],
             pltpu.VMEM((n, 1, LANES), f32),
+            pltpu.VMEM((MAXNB, SPAN, width), bf16),
             pltpu.VMEM((width // LANES, n * cv, LANES), f32),
             pltpu.VMEM((width // LANES, n * cv, LANES), f32),
-            pltpu.VMEM((n, cv, width), i16),
-            pltpu.VMEM((n, 1, LANES), f32),
-            pltpu.VMEM((n, cv, width), i16),
-            pltpu.VMEM((n, 1, LANES), f32),
+            *[pltpu.VMEM((n, rows, width), i16) for _, rows in CHUNKS],
+            pltpu.VMEM((len(CHUNKS), n, 1, LANES), f32),
+            *[pltpu.VMEM((n, rows, width), i16) for _, rows in CHUNKS],
+            pltpu.VMEM((len(CHUNKS), n, 1, LANES), f32),
             sem((1,)), sem((1,)),
             sem((1,)), sem((1,)),
             sem((1,)), sem((ROUNDS,)),
+            sem((2,)), sem((2,)),
             sem((1,)), sem((1,)),
-            sem((1,)), sem((1,)),
-            sem((1,)), sem((ROUNDS,)),
-            sem((1,)), sem((ROUNDS,)),
-            sem((n // 16,)), sem((1,)),
+            sem((2,)), sem((2, ROUNDS)),
+            sem((2,)), sem((2, ROUNDS)),
+            sem((n // 16,)), sem((1,)), sem((5,)),
         ],
         compiler_params=pltpu.CompilerParams(
-            collective_id=1, has_side_effects=True, vmem_limit_bytes=50 << 20
+            collective_id=1, has_side_effects=True, vmem_limit_bytes=44 << 20
         ),
         name="whole",
     )(col_slot, col_pos, request, owners, prolong, stiffness)

time: 107 us -> 98.4 us (0.920)
  Pallas kernels: 98 us -> 92.3 us
  local copies, waits for them, and re-layouts: 8.49 us -> 5.86 us
    pallas_call x1, Pallas kernels: 98 us -> 92.3 us  [whole(): pl.pallas_call(whole_kernel, out_shape=jax.ShapeDtypeStruct((n, cv, width...]
    unnamed x11, local copies, waits for them, and re-layouts: 8.49 us -> 5.86 us
where the time goes in v3:
time: 98.4 us; the launch traced here: 98.2 us
  Pallas kernels  92.3 us (94%)
  local copies, waits for them, and re-layouts  5.86 us (6%)
    pallas_call x1, Pallas kernels, whole(): pl.pallas_call(whole_kernel, out_shape=jax.ShapeDtypeStruct((n, cv, width...  92.3 us
    unnamed x11, local copies, waits for them, and re-layouts  5.86 us

profile of v3, /device:TPU:1, one launch (start us, length us, event | category | flops | bytes accessed | tf_op | source)
XLA Modules:
  0.0 98.2 jit_solution(18093019128409406650)
XLA Ops:
  0.0 0.0 copy-start
  0.0 1.0 %copy-done = bf16[64,24,128]{2,1,0:T(8,128)(2,1)S(1)} copy-done((bf16[64,24,128]{2,1,0:T(8,128)(2,1)S(1)}, bf16[64,24,128]{2,1,0:T(8,128)(2,1)}, u32[]{:S(2)}) %copy-start) | copy-done | bytes 393240
  1.0 0.0 copy-start.1
  1.0 0.7 copy-done.1
  1.7 0.0 copy-start.2
  1.7 0.7 copy-done.2
  2.4 0.0 copy-start.3
  2.4 0.7 copy-done.3
  3.0 0.0 copy-start.4
  3.0 0.7 copy-done.4
  3.7 92.3 %whole.1 = f32[128,24,384]{2,1,0:T(8,128)S(1)} custom-call(s32[4,128]{1,0:T(4,128)S(1)} %bitcast.3, s32[4,128]{1,0:T(4,128)S(1)} %bitcast.4, s32[128]{0:T(128)S(1)} %copy-done.3, s32[64]{0:T(128)S(1)} %bitcast.5, bf16[64,24,128]{2,1,0:T(8,128)(2,1)S(1)} %copy-done, bf16[128,4,128,128]{3,2,1,0:T(8,128)(2,1)} %stiff_ref.1), custom_call_target="tpu_custom_call" | custom-call | tf_op jit(solution)/shard_map/whole/pallas_call | solution.py:400
  96.0 2.2 %copy.8 = f32[128,24,384]{2,1,0:T(8,128)} copy(f32[128,24,384]{2,1,0:T(8,128)S(1)} %whole.1) | data formatting | bytes 9437184
Async XLA Ops:
  0.0 1.0 %copy-start = (bf16[64,24,128]{2,1,0:T(8,128)(2,1)S(1)}, bf16[64,24,128]{2,1,0:T(8,128)(2,1)}, u32[]{:S(2)}) copy-start(bf16[64,24,128]{2,1,0:T(8,128)(2,1)} %prolong_in.1) | copy-start | bytes 1179652
  1.0 0.7 copy-start.1
  1.7 0.7 copy-start.2
  2.4 0.7 copy-start.3
  3.0 0.7 copy-start.4

commit v4 on v3

--- a/solution.py
+++ b/solution.py
@@ -11,6 +11,7 @@
 AXES = ("gx", "gy")
 LANES = 128
 SPAN = 32
+PITCH = 28
 CHUNKS = ((0, 8), (8, 16))
 ROUNDS = 16
 WIDE = 8
@@ -54,7 +55,7 @@
     slot_in, pos_in, ask_in, owner_in, prolong_in, stiff_ref,
     out_ref,
     slot_ref, pos_ref, ask_ref, owner_ref, prolong_ref,
-    meta_ref, mid_ref, meta_in, req_ref, stage_ref, fetched_ref, mats_ref, pk_ref, cols_ref,
+    meta_ref, mid_ref, req_ref, stage_ref, fetched_ref, mats_ref, pk_ref, cols_ref,
     code_a, code_b, factor_ref, part_a, part_b, scale_ref, table_ref, spread_ref, total_ref,
     rows_a, rows_b, rows_scale, land_a, land_b, land_scale,
     near_send, near_recv, far_send, far_recv, fetch_send, fetch_recv, part_send, part_recv, fact_send, fact_recv,
@@ -154,17 +155,16 @@
     bulk(meta_ref, mid_ref, near_send.at[0], near_recv.at[0], 7).wait()
     for where in far:
         remote(
-            mid_ref.at[:, where[1]], meta_in.at[:, gy], far_send.at[0], far_recv.at[0], where
-        ).start()
-    meta_in[:, gy] = mid_ref[:, gy]
+            mid_ref.at[:, where[1]], req_ref.at[:, gy], far_send.at[0], far_recv.at[0], where
+        ).start()
+    to_scalars = pltpu.make_async_copy(mid_ref.at[:, gy], req_ref.at[:, gy], req_sem.at[0])
+    to_scalars.start()
     remote(
-        mid_ref.at[:, pl.ds(0, 15)], meta_in.at[:, pl.ds(0, 15)],
+        mid_ref.at[:, pl.ds(0, 15)], req_ref.at[:, pl.ds(0, 15)],
         far_send.at[0], far_recv.at[0], (gx, gy),
     ).wait()
     for copy in small[2:]:
         copy.wait()
-    to_scalars = pltpu.make_async_copy(meta_in, req_ref, req_sem.at[0])
-    to_scalars.start()
     to_scalars.wait()
 
     def asked(d, k):
@@ -292,10 +292,10 @@
         moved = jnp.dot(both, units, preferred_element_type=jnp.float32)
         moved = moved[:rows] + moved[rows:]
         for k in range(tiles):
-            spread_ref[k, pl.ds(d * cv + first, rows), :] = moved[:, LANES * k : LANES * (k + 1)]
+            spread_ref[k, pl.ds(d * PITCH + first, rows), :] = moved[:, LANES * k : LANES * (k + 1)]
 
     def combine(c, carry):
-        at = pl.ds(c, n, stride=cv)
+        at = pl.ds(c, n, stride=PITCH)
         every = jnp.concatenate([spread_ref[k, at, :] for k in range(tiles)], axis=1)
         total = jnp.dot(
             hot, jnp.concatenate(split(every), axis=0), preferred_element_type=jnp.float32
@@ -321,7 +321,7 @@
 
         def encode(o):
             row = jnp.concatenate(
-                [total_ref[k, pl.ds(o * cv + first, rows), :] for k in range(tiles)], axis=1
+                [total_ref[k, pl.ds(o * PITCH + first, rows), :] for k in range(tiles)], axis=1
             )
             code, factor = coded(row)
             rows_ref[o] = code.astype(jnp.int16)
@@ -410,7 +410,6 @@
             pltpu.VMEM(prolong.shape, bf16),
             pltpu.VMEM((8, 16, 1, LANES), i32),
             pltpu.VMEM((8, 16, 1, LANES), i32),
-            pltpu.VMEM((8, 16, 1, LANES), i32),
             pltpu.SMEM((8, 16, 1, LANES), i32),
             pltpu.VMEM((n, cv, dof), bf16),
             pltpu.VMEM((n, cv, dof), bf16),
@@ -422,8 +421,8 @@
             *[pltpu.VMEM((n, rows, LANES), i16) for _, rows in CHUNKS],
             pltpu.VMEM((n, 1, LANES), f32),
             pltpu.VMEM((MAXNB, SPAN, width), bf16),
-            pltpu.VMEM((width // LANES, n * cv, LANES), f32),
-            pltpu.VMEM((width // LANES, n * cv, LANES), f32),
+            pltpu.VMEM((width // LANES, n * PITCH, LANES), f32),
+            pltpu.VMEM((width // LANES, n * PITCH, LANES), f32),
             *[pltpu.VMEM((n, rows, width), i16) for _, rows in CHUNKS],
             pltpu.VMEM((len(CHUNKS), n, 1, LANES), f32),
             *[pltpu.VMEM((n, rows, width), i16) for _, rows in CHUNKS],
@@ -438,10 +437,15 @@
             sem((n // 16,)), sem((1,)), sem((5,)),
         ],
         compiler_params=pltpu.CompilerParams(
-            collective_id=1, has_side_effects=True, vmem_limit_bytes=44 << 20
+            collective_id=1, has_side_effects=True, vmem_limit_bytes=46 << 20
         ),
         name="whole",
-    )(col_slot, col_pos, request, owners, prolong, stiffness)
+    )(
+        *[
+            pltpu.with_memory_space_constraint(a, pltpu.HBM)
+            for a in (col_slot, col_pos, request, owners, prolong, stiffness)
+        ]
+    )
 
 
 def per_device(prolong, stiffness, request, col_slot, col_pos, coarse_owner):

time: 98.4 us -> 92.2 us (0.937)
  local copies, waits for them, and re-layouts: 5.86 us -> 2.19 us
  Pallas kernels: 92.3 us -> 89.9 us
    unnamed x11 -> x1, local copies, waits for them, and re-layouts: 5.86 us -> 2.19 us
    pallas_call x1, Pallas kernels: 92.3 us -> 89.9 us  [whole(): pl.pallas_call(whole_kernel, out_shape=jax.ShapeDtypeStruct((n, cv, width...]
where the time goes in v4:
time: 92.2 us; the launch traced here: 92.1 us
  Pallas kernels  89.9 us (98%)
  local copies, waits for them, and re-layouts  2.19 us (2%)
    pallas_call x1, Pallas kernels, whole(): pl.pallas_call(whole_kernel, out_shape=jax.ShapeDtypeStruct((n, cv, width...  89.9 us
    unnamed x1, local copies, waits for them, and re-layouts  2.19 us

profile of v4, /device:TPU:1, one launch (start us, length us, event | category | flops | bytes accessed | tf_op | source)
XLA Modules:
  0.0 92.1 jit_solution(966302723674448414)
XLA Ops:
  0.0 89.9 %whole.1 = f32[128,24,384]{2,1,0:T(8,128)S(1)} custom-call(s32[4,128]{1,0:T(4,128)} %bitcast.3, s32[4,128]{1,0:T(4,128)} %bitcast.4, s32[128]{0:T(128)} %ask_in.1, s32[64]{0:T(128)} %bitcast.5, bf16[64,24,128]{2,1,0:T(8,128)(2,1)} %prolong_in.1, bf16[128,4,128,128]{3,2,1,0:T(8,128)(2,1)} %stiff_ref.1), custom_call_target="tpu_custom_call" | custom-call | tf_op jit(solution)/shard_map/whole/pallas_call | solution.py:400
  89.9 2.2 %copy.8 = f32[128,24,384]{2,1,0:T(8,128)} copy(f32[128,24,384]{2,1,0:T(8,128)S(1)} %whole.1) | data formatting | bytes 9437184

commit v5 on v4

--- a/solution.py
+++ b/solution.py
@@ -13,8 +13,10 @@
 SPAN = 32
 PITCH = 28
 CHUNKS = ((0, 8), (8, 16))
-ROUNDS = 16
-WIDE = 8
+ROUNDS = 8
+WIDE = 16
+COLS = 8
+ROLLED = 4
 TOP = 32767.0
 MESH = pl.DeviceIdType.MESH
 HBM = pl.BlockSpec(memory_space=pltpu.HBM)
@@ -68,26 +70,32 @@
     me = gx * 16 + gy
     z, core = gx // 2, lax.rem(gx, 2)
     x, y = gy // 4, lax.rem(gy, 4)
-    to_gx = [lax.rem(z + j // 2, 4) * 2 + lax.rem(core + j, 2) for j in range(WIDE)]
-    from_gx = [lax.rem(z + 4 - j // 2, 4) * 2 + lax.rem(core + j, 2) for j in range(WIDE)]
-
-    def target(i, j):
-        s = lax.rem(i * 5 + j * 3, 16)
-        return to_gx[j], lax.rem(x + s // 4, 4) * 4 + lax.rem(y + s, 4)
-
-    def source(i, j):
-        s = lax.rem(i * 5 + j * 3, 16)
-        return from_gx[j] * 16 + lax.rem(x + 4 - s // 4, 4) * 4 + lax.rem(y + 16 - s, 4)
+    to_gy = [lax.rem(x + s // 4, 4) * 4 + lax.rem(y + s % 4, 4) for s in range(WIDE)]
+    from_gy = [lax.rem(x + 4 - s // 4, 4) * 4 + lax.rem(y + 4 - s % 4, 4) for s in range(WIDE)]
+
+    def shift(r):
+        t = r // 2
+        dz = 2 + t - 3 * (t // 2) - 2 * (t // 3)
+        other = lax.rem(core + 1 + r, 2)
+        return lax.rem(z + dz, 4) * 2 + other, lax.rem(z + 4 - dz, 4) * 2 + other
+
+    def targets(r):
+        row, _ = shift(r)
+        return [(row, to_gy[s]) for s in range(WIDE)]
+
+    def sources(r):
+        _, row = shift(r)
+        return [row * 16 + from_gy[s] for s in range(WIDE)]
 
     def each(fn):
-        def body(i, c):
-            for j in range(WIDE):
-                fn(i, j)
+        def body(r, c):
+            for where in targets(r):
+                fn(r, where)
             return c
 
-        for j in range(1, WIDE):
-            fn(0, j)
-        lax.fori_loop(1, ROUNDS, body, 0)
+        lax.fori_loop(0, ROUNDS - 1, body, 0)
+        for where in targets(ROUNDS - 1)[1:]:
+            fn(ROUNDS - 1, where)
 
     def remote(src, dst, send_sem, recv_sem, where):
         return pltpu.make_async_remote_copy(
@@ -121,8 +129,8 @@
         copy.start()
 
     barrier = pltpu.get_barrier_semaphore()
-    near = [(g, gy) for g in to_gx[1:]]
-    far = [(gx, lax.rem(x + s // 4, 4) * 4 + lax.rem(y + s, 4)) for s in range(1, 16)]
+    near = [(shift(r)[0], gy) for r in range(ROUNDS - 1)]
+    far = [(gx, g) for g in to_gy[1:]]
     for where in near + far:
         pl.semaphore_signal(barrier, inc=1, device_id=where, device_id_type=MESH)
 
@@ -167,24 +175,21 @@
         copy.wait()
     to_scalars.wait()
 
-    def asked(d, k):
-        return req_ref[d // 16, lax.rem(d, 16), 0, k]
-
-    def fill(p, c):
-        stage_ref[p] = prolong_ref[asked(p, 0)]
+    def fill(g, c):
+        for h in range(16):
+            stage_ref[g * 16 + h] = prolong_ref[req_ref[g, h, 0, 0]]
         return c
 
-    lax.fori_loop(0, n, fill, 0, unroll=8)
-
-    def answer(i, j):
-        where = target(i, j)
+    lax.fori_loop(0, 8, fill, 0)
+
+    def answer(r, where):
         remote(
             stage_ref.at[where[0] * 16 + where[1]], fetched_ref.at[me],
-            fetch_send.at[0], fetch_recv.at[i], where,
+            fetch_send.at[0], fetch_recv.at[r], where,
         ).start()
 
     each(answer)
-    fetched_ref[me] = prolong_ref[asked(me, 0)]
+    fetched_ref[me] = prolong_ref[req_ref[gx, gy, 0, 0]]
     for copy in loads:
         copy.wait()
 
@@ -199,18 +204,18 @@
         pk_ref[t, :, 0:dof] = hi
         pk_ref[t, :, dof : 2 * dof] = lo
 
-    bulk(stage_ref, fetched_ref, fetch_send.at[0], fetch_recv.at[0], WIDE - 1).wait_recv()
-    left_product(me)
-    for j in range(1, WIDE):
-        left_product(source(0, j))
-
-    def take(i, c):
-        bulk(stage_ref, fetched_ref, fetch_send.at[0], fetch_recv.at[i], WIDE).wait_recv()
-        for j in range(WIDE):
-            left_product(source(i, j))
+    def take(r, c):
+        bulk(stage_ref, fetched_ref, fetch_send.at[0], fetch_recv.at[r], WIDE).wait_recv()
+        for t in sources(r):
+            left_product(t)
         return c
 
-    lax.fori_loop(1, ROUNDS, take, 0)
+    lax.fori_loop(0, ROUNDS - 1, take, 0)
+    bulk(
+        stage_ref, fetched_ref, fetch_send.at[0], fetch_recv.at[ROUNDS - 1], WIDE - 1
+    ).wait_recv()
+    for t in sources(ROUNDS - 1):
+        left_product(t)
 
     lane = lax.broadcasted_iota(jnp.int32, (cv, LANES), 1)
 
@@ -228,8 +233,7 @@
             ref[t] = code[first : first + rows].astype(jnp.int16)
         factor_ref[t] = as_row(factor)
 
-    def give(i, j):
-        where = target(i, j)
+    def give(where):
         peer = where[0] * 16 + where[1]
         remote(
             factor_ref.at[peer], scale_ref.at[me], fact_send.at[0], fact_recv.at[0], where
@@ -238,42 +242,37 @@
             code_a.at[peer], part_a.at[me], part_send.at[0], part_recv.at[0], where
         ).start()
 
-    def give_rest(i, j):
-        where = target(i, j)
+    def give_rest(r, where):
         remote(
             code_b.at[where[0] * 16 + where[1]], part_b.at[me],
             part_send.at[1], part_recv.at[1], where,
         ).start()
 
-    def index(i, j):
-        where = target(i, j)
-        return where[0] * 16 + where[1]
-
-    for j in range(WIDE):
-        right_product(index(0, j), j)
-
-    def work(i, c):
-        for j in range(WIDE):
-            right_product(index(i, j), j)
-
-        for j in range(WIDE):
-            @pl.when((i > 1) | (j > 0))
-            def _():
-                give(i - 1, j)
+    def multiply(r):
+        for s, where in enumerate(targets(r)):
+            right_product(where[0] * 16 + where[1], s % COLS)
+
+    def work(r, c):
+        multiply(r)
+        for where in targets(r - 1):
+            give(where)
         return c
 
+    multiply(0)
     lax.fori_loop(1, ROUNDS, work, 0)
-    for j in range(WIDE):
-        give(ROUNDS - 1, j)
+    for where in targets(ROUNDS - 1)[1:]:
+        give(where)
     each(give_rest)
     part_a[me] = code_a[me]
     part_b[me] = code_b[me]
     scale_ref[me] = factor_ref[me]
 
-    def locate(d, row):
-        return jnp.where(row_lane == d, owner_ref[asked(d, 0)], row)
-
-    place = lax.fori_loop(0, n, locate, jnp.zeros((1, LANES), jnp.int32), unroll=8)
+    def locate(g, row):
+        for h in range(16):
+            row = jnp.where(row_lane == g * 16 + h, owner_ref[req_ref[g, h, 0, 0]], row)
+        return row
+
+    place = lax.fori_loop(0, 8, locate, jnp.zeros((1, LANES), jnp.int32))
     hot = jnp.where(
         lax.broadcasted_iota(jnp.int32, (n, LANES), 0) == place, 1.0, 0.0
     ).astype(jnp.bfloat16)
@@ -281,18 +280,28 @@
 
     tiles = width // LANES
 
-    def spread(part, first, rows, d):
+    lane_row = lax.broadcasted_iota(jnp.int32, (1, LANES), 1)
+    blocks = [(lane_row + LANES * k) // cv for k in range(tiles)]
+
+    def spread(part, first, rows, g, h):
+        d = g * 16 + h
         values = part[d].astype(jnp.int32).astype(jnp.float32)
         values = values * as_column(scale_ref[d], rows, first)
-        hi = values.astype(jnp.bfloat16).astype(jnp.float32)
-        both = jnp.concatenate([hi, values - hi], axis=0).astype(jnp.bfloat16)
-        units = jnp.concatenate(
-            [table_ref[asked(d, 1 + q)] for q in range(bps)], axis=0
-        )
-        moved = jnp.dot(both, units, preferred_element_type=jnp.float32)
-        moved = moved[:rows] + moved[rows:]
+        pos = [req_ref[g, h, 0, 1 + q] for q in range(bps)]
+        if h % ROLLED:
+            hi = values.astype(jnp.bfloat16).astype(jnp.float32)
+            both = jnp.concatenate([hi, values - hi], axis=0).astype(jnp.bfloat16)
+            units = jnp.concatenate([table_ref[p] for p in pos], axis=0)
+            moved = jnp.dot(both, units, preferred_element_type=jnp.float32)
+            moved = moved[:rows] + moved[rows:]
+            moved = [moved[:, LANES * k : LANES * (k + 1)] for k in range(tiles)]
+        else:
+            moved = [jnp.zeros((rows, LANES), jnp.float32)] * tiles
+            for q, p in enumerate(pos):
+                turned = pltpu.roll(values, lax.rem(p * cv - SPAN * q + LANES, LANES), 1)
+                moved = [jnp.where(k == p, turned, m) for k, m in zip(blocks, moved)]
         for k in range(tiles):
-            spread_ref[k, pl.ds(d * PITCH + first, rows), :] = moved[:, LANES * k : LANES * (k + 1)]
+            spread_ref[k, pl.ds(d * PITCH + first, rows), :] = moved[k]
 
     def combine(c, carry):
         at = pl.ds(c, n, stride=PITCH)
@@ -311,12 +320,12 @@
         if h == 0:
             bulk(factor_ref, scale_ref, fact_send.at[0], fact_recv.at[0], n - 1).wait()
 
-        def spread_some(i, c):
-            for j in range(WIDE):
-                spread(part, first, rows, i * WIDE + j)
+        def spread_some(g, c):
+            for j in range(16):
+                spread(part, first, rows, g, j)
             return c
 
-        lax.fori_loop(0, ROUNDS, spread_some, 0)
+        lax.fori_loop(0, 8, spread_some, 0)
         lax.fori_loop(first, first + rows, combine, 0)
 
         def encode(o):
@@ -327,33 +336,31 @@
             rows_ref[o] = code.astype(jnp.int16)
             rows_scale[h, o] = as_row(factor, first)
 
-        def deliver(i, j):
-            where = target(i, j)
+        def deliver(r, where):
             peer = where[0] * 16 + where[1]
             remote(
                 rows_scale.at[h, peer], land_scale.at[h, me],
-                rsc_send.at[h], rsc_recv.at[h, i], where,
+                rsc_send.at[h], rsc_recv.at[h, r], where,
             ).start()
             remote(
                 rows_ref.at[peer], land_ref.at[me],
-                rows_send.at[h], rows_recv.at[h, i], where,
+                rows_send.at[h], rows_recv.at[h, r], where,
             ).start()
 
-        for j in range(WIDE):
-            encode(index(0, j))
-
-        def emit(i, c):
-            for j in range(WIDE):
-                encode(index(i, j))
-            for j in range(WIDE):
-                @pl.when((i > 1) | (j > 0))
-                def _():
-                    deliver(i - 1, j)
+        def encode_all(r):
+            for where in targets(r):
+                encode(where[0] * 16 + where[1])
+
+        def emit(r, c):
+            encode_all(r)
+            for where in targets(r - 1):
+                deliver(r - 1, where)
             return c
 
+        encode_all(0)
         lax.fori_loop(1, ROUNDS, emit, 0)
-        for j in range(WIDE):
-            deliver(ROUNDS - 1, j)
+        for where in targets(ROUNDS - 1)[1:]:
+            deliver(ROUNDS - 1, where)
 
     for h, ((first, rows), rows_ref, land_ref) in enumerate(
         zip(CHUNKS, (rows_a, rows_b), (land_a, land_b))
@@ -370,19 +377,17 @@
             ).wait_recv()
 
         decode(rows_ref[me], rows_scale[h, me], me)
-        arrived(0, WIDE - 1)
-        for j in range(1, WIDE):
-            p = source(0, j)
-            decode(land_ref[p], land_scale[h, p], p)
-
-        def drain(i, c):
-            arrived(i, WIDE)
-            for j in range(WIDE):
-                p = source(i, j)
+
+        def drain(r, c):
+            arrived(r, WIDE)
+            for p in sources(r):
                 decode(land_ref[p], land_scale[h, p], p)
             return c
 
-        lax.fori_loop(1, ROUNDS, drain, 0)
+        lax.fori_loop(0, ROUNDS - 1, drain, 0)
+        arrived(ROUNDS - 1, WIDE - 1)
+        for p in sources(ROUNDS - 1)[1:]:
+            decode(land_ref[p], land_scale[h, p], p)
         bulk(rows_ref, land_ref, rows_send.at[h], rows_recv.at[h, 0], n - 1).wait_send()
         bulk(
             rows_scale.at[h], land_scale.at[h], rsc_send.at[h], rsc_recv.at[h, 0], n - 1
@@ -415,7 +420,7 @@
             pltpu.VMEM((n, cv, dof), bf16),
             pltpu.VMEM(stiffness.shape, bf16),
             pltpu.VMEM((n, bps * cv, 2 * dof), bf16),
-            pltpu.VMEM((WIDE, LANES, 2 * dof), bf16),
+            pltpu.VMEM((COLS, LANES, 2 * dof), bf16),
             *[pltpu.VMEM((n, rows, LANES), i16) for _, rows in CHUNKS],
             pltpu.VMEM((n, 1, LANES), f32),
             *[pltpu.VMEM((n, rows, LANES), i16) for _, rows in CHUNKS],

time: 92.2 us -> 88.3 us (0.958)
  Pallas kernels: 89.9 us -> 86.1 us
    pallas_call x1, Pallas kernels: 89.9 us -> 86.1 us  [whole(): pl.pallas_call(whole_kernel, out_shape=jax.ShapeDtypeStruct((n, cv, width...]
where the time goes in v5:
time: 88.3 us
  Pallas kernels  86.1 us (98%)
  local copies, waits for them, and re-layouts  2.19 us (2%)
    pallas_call x1, Pallas kernels, whole(): pl.pallas_call(whole_kernel, out_shape=jax.ShapeDtypeStruct((n, cv, width...  86.1 us
    unnamed x1, local copies, waits for them, and re-layouts  2.19 us

profile of v5, /device:TPU:1, one launch (start us, length us, event | category | flops | bytes accessed | tf_op | source)
XLA Modules:
  0.0 88.3 jit_solution(2586785899142314074)
XLA Ops:
  0.0 86.1 %whole.1 = f32[128,24,384]{2,1,0:T(8,128)S(1)} custom-call(s32[4,128]{1,0:T(4,128)} %bitcast.3, s32[4,128]{1,0:T(4,128)} %bitcast.4, s32[128]{0:T(128)} %ask_in.1, s32[64]{0:T(128)} %bitcast.5, bf16[64,24,128]{2,1,0:T(8,128)(2,1)} %prolong_in.1, bf16[128,4,128,128]{3,2,1,0:T(8,128)(2,1)} %stiff_ref.1), custom_call_target="tpu_custom_call" | custom-call | tf_op jit(solution)/shard_map/whole/pallas_call | solution.py:405
  86.1 2.2 %copy.8 = f32[128,24,384]{2,1,0:T(8,128)} copy(f32[128,24,384]{2,1,0:T(8,128)S(1)} %whole.1) | data formatting | bytes 9437184

commit v6 on v5

--- a/solution.py
+++ b/solution.py
@@ -74,9 +74,9 @@
     from_gy = [lax.rem(x + 4 - s // 4, 4) * 4 + lax.rem(y + 4 - s % 4, 4) for s in range(WIDE)]
 
     def shift(r):
-        t = r // 2
-        dz = 2 + t - 3 * (t // 2) - 2 * (t // 3)
-        other = lax.rem(core + 1 + r, 2)
+        u = r % 4
+        dz = 2 - u + 3 * (u // 2) - 2 * (u // 3)
+        other = lax.rem(core + 1 + u % 2 - u // 3 + r // 4, 2)
         return lax.rem(z + dz, 4) * 2 + other, lax.rem(z + 4 - dz, 4) * 2 + other
 
     def targets(r):

time: 88.3 us -> 81.6 us (0.924)
  Pallas kernels: 86.1 us -> 79.5 us
    pallas_call x1, Pallas kernels: 86.1 us -> 79.5 us  [whole(): pl.pallas_call(whole_kernel, out_shape=jax.ShapeDtypeStruct((n, cv, width...]
where the time goes in v6:
time: 81.6 us; the launch traced here: 81.7 us
  Pallas kernels  79.5 us (97%)
  local copies, waits for them, and re-layouts  2.19 us (3%)
    pallas_call x1, Pallas kernels, whole(): pl.pallas_call(whole_kernel, out_shape=jax.ShapeDtypeStruct((n, cv, width...  79.5 us
    unnamed x1, local copies, waits for them, and re-layouts  2.19 us

profile of v6, /device:TPU:1, one launch (start us, length us, event | category | flops | bytes accessed | tf_op | source)
XLA Modules:
  0.0 81.7 jit_solution(4815951119021643496)
XLA Ops:
  0.0 79.5 %whole.1 = f32[128,24,384]{2,1,0:T(8,128)S(1)} custom-call(s32[4,128]{1,0:T(4,128)} %bitcast.3, s32[4,128]{1,0:T(4,128)} %bitcast.4, s32[128]{0:T(128)} %ask_in.1, s32[64]{0:T(128)} %bitcast.5, bf16[64,24,128]{2,1,0:T(8,128)(2,1)} %prolong_in.1, bf16[128,4,128,128]{3,2,1,0:T(8,128)(2,1)} %stiff_ref.1), custom_call_target="tpu_custom_call" | custom-call | tf_op jit(solution)/shard_map/whole/pallas_call | solution.py:405
  79.5 2.2 %copy.8 = f32[128,24,384]{2,1,0:T(8,128)} copy(f32[128,24,384]{2,1,0:T(8,128)S(1)} %whole.1) | data formatting | bytes 9437184

commit v7 on v6

--- a/solution.py
+++ b/solution.py
@@ -15,6 +15,7 @@
 CHUNKS = ((0, 8), (8, 16))
 ROUNDS = 8
 WIDE = 16
+TURNS = (0, 7, 14, 5, 12, 3, 10, 1, 8, 15, 6, 13, 4, 11, 2, 9)
 COLS = 8
 ROLLED = 4
 TOP = 32767.0
@@ -70,8 +71,8 @@
     me = gx * 16 + gy
     z, core = gx // 2, lax.rem(gx, 2)
     x, y = gy // 4, lax.rem(gy, 4)
-    to_gy = [lax.rem(x + s // 4, 4) * 4 + lax.rem(y + s % 4, 4) for s in range(WIDE)]
-    from_gy = [lax.rem(x + 4 - s // 4, 4) * 4 + lax.rem(y + 4 - s % 4, 4) for s in range(WIDE)]
+    to_gy = [lax.rem(x + s // 4, 4) * 4 + lax.rem(y + s % 4, 4) for s in TURNS]
+    from_gy = [lax.rem(x + 4 - s // 4, 4) * 4 + lax.rem(y + 4 - s % 4, 4) for s in TURNS]
 
     def shift(r):
         u = r % 4
@@ -426,8 +427,8 @@
             *[pltpu.VMEM((n, rows, LANES), i16) for _, rows in CHUNKS],
             pltpu.VMEM((n, 1, LANES), f32),
             pltpu.VMEM((MAXNB, SPAN, width), bf16),
-            pltpu.VMEM((width // LANES, n * PITCH, LANES), f32),
-            pltpu.VMEM((width // LANES, n * PITCH, LANES), f32),
+            pltpu.VMEM((width // LANES, (n + 1) * PITCH, LANES), f32),
+            pltpu.VMEM((width // LANES, (n + 1) * PITCH, LANES), f32),
             *[pltpu.VMEM((n, rows, width), i16) for _, rows in CHUNKS],
             pltpu.VMEM((len(CHUNKS), n, 1, LANES), f32),
             *[pltpu.VMEM((n, rows, width), i16) for _, rows in CHUNKS],

time: 81.6 us -> 80.6 us (0.988)
  Pallas kernels: 79.5 us -> 78.3 us
    pallas_call x1, Pallas kernels: 79.5 us -> 78.3 us  [whole(): pl.pallas_call(whole_kernel, out_shape=jax.ShapeDtypeStruct((n, cv, width...]
where the time goes in v7:
time: 80.6 us; the launch traced here: 80.5 us
  Pallas kernels  78.3 us (97%)
  local copies, waits for them, and re-layouts  2.19 us (3%)
    pallas_call x1, Pallas kernels, whole(): pl.pallas_call(whole_kernel, out_shape=jax.ShapeDtypeStruct((n, cv, width...  78.3 us
    unnamed x1, local copies, waits for them, and re-layouts  2.19 us

profile of v7, /device:TPU:1, one launch (start us, length us, event | category | flops | bytes accessed | tf_op | source)
XLA Modules:
  0.0 80.5 jit_solution(2510639380431689523)
XLA Ops:
  0.0 78.3 %whole.1 = f32[128,24,384]{2,1,0:T(8,128)S(1)} custom-call(s32[4,128]{1,0:T(4,128)} %bitcast.3, s32[4,128]{1,0:T(4,128)} %bitcast.4, s32[128]{0:T(128)} %ask_in.1, s32[64]{0:T(128)} %bitcast.5, bf16[64,24,128]{2,1,0:T(8,128)(2,1)} %prolong_in.1, bf16[128,4,128,128]{3,2,1,0:T(8,128)(2,1)} %stiff_ref.1), custom_call_target="tpu_custom_call" | custom-call | tf_op jit(solution)/shard_map/whole/pallas_call | solution.py:406
  78.3 2.2 %copy.8 = f32[128,24,384]{2,1,0:T(8,128)} copy(f32[128,24,384]{2,1,0:T(8,128)S(1)} %whole.1) | data formatting | bytes 9437184
